TPU v7x, 32 devices: a whole 2x2x4 slice. The times are simulated.
32 devices in a mesh: seq: 8 (over z, x), head: 4 (over y, core).
Axes of the slice: x: 2, y: 2, z: 4, core: 2. Of those that a mesh axis runs over, the one named last changes fastest.
Arguments:
- queries: bfloat16 [8192, 4096], P('seq', 'head'), may hold values from -8 to 8
- key_rows: bfloat16 [8192, 4096], P('seq', 'head'), may hold values from -8 to 8
- value_rows: bfloat16 [8192, 4096], P('seq', 'head'), may hold values from -6 to 6
- random_owner: int32 [128, 3], P('seq'), may hold values from 0 to 7, all different within a row; in each aligned block of 16 rows (0 to 15, 16 to 31, ...) at most 8 rows name the same one
- random_local: int32 [128, 3], P('seq'), may hold values from 0 to 15
- output_weight: bfloat16 [4096, 4096], P('head'), may hold values from -0.09375 to 0.09375
Outputs:
- layer_output: bfloat16 [8192, 4096], P(('seq', 'head'))
Inputs may be any that keep to these rules, and one draw needn't show every extreme that they name: `random_owner`: each row names 3 different owners. Among the rows of one device (16 aligned rows) no owner is named more than 8 times, and in some device's rows one owner is named exactly 8 times.
All inputs are finite; a program needn't handle non-finite values.
Results may differ from a plain program's by a relative error of at most 0.0052.
Values may be sent and summed in bfloat16 or wider, within the bound.
No kernel may reach another device: no remote copies, remote signals or barrier semaphores. Data moves between devices by JAX's collectives and lax.ppermute only.
A program may use at most 192 MiB of HBM per device.

v0:
```python
import math

import jax
import jax.numpy as jnp
from jax import lax
from jax.sharding import PartitionSpec as P

HEAD_DIM = 128
BLOCK = 64
RANDOM = 3
GLOBAL = 128


masked_score = -1e30


def padded(array, sides, width):
    for axis, dim in sides:
        peers, length = (lax.axis_size(axis), array.shape[dim])
        up = [(i, (i + 1) % peers) for i in range(peers - 1)]
        down = [(j, i) for i, j in up]
        last = lax.slice_in_dim(array, length - width, length, axis=dim)
        first = lax.slice_in_dim(array, 0, width, axis=dim)
        before = lax.ppermute(last, axis, up)
        after = lax.ppermute(first, axis, down)
        array = jnp.concatenate([before, array, after], axis=dim)
    return array


def from_root(block, axis, holder):
    block = jnp.where(lax.axis_index(axis) == holder, block, jnp.zeros_like(block))
    return lax.psum(block, axis)


def combined_all(array, axis, combine):
    everything = jax.tree.map(lambda part: lax.all_gather(part, axis), array)
    first = jax.tree.map(lambda part: part[0], everything)

    def lap(k, so_far):
        return combine(so_far, jax.tree.map(lambda part: part[k], everything))

    return lax.fori_loop(1, lax.axis_size(axis), lap, first)


def slot_table(owner_ids, local_ids, seq_count, slot_count):
    owner_hits = (owner_ids[:, None] == jnp.arange(seq_count, dtype=jnp.int32)[None, :]).astype(
        jnp.int32
    )
    earlier = jnp.cumsum(owner_hits, axis=0) - owner_hits
    slot_ids = jnp.sum(earlier * owner_hits, axis=1)
    slot_hits = (slot_ids[:, None] == jnp.arange(slot_count, dtype=jnp.int32)[None, :]).astype(
        jnp.int32
    )
    request_table = jnp.sum(
        (owner_hits * local_ids[:, None])[:, :, None] * slot_hits[:, None, :], axis=0
    )
    return (request_table, slot_ids)


def local(queries, key_rows, value_rows, random_owner, random_local, output_weight):
    seq_count = lax.axis_size("seq")
    seq_index = lax.axis_index("seq")
    token_count, width_here = queries.shape
    blocks_here = token_count // BLOCK
    heads_here = width_here // HEAD_DIM
    slot_count = max(2, 4 * blocks_here // seq_count)
    total_blocks = seq_count * blocks_here
    score_scale = HEAD_DIM ** (-0.5)
    key_blocks = key_rows.reshape(blocks_here, BLOCK, width_here)
    value_blocks = value_rows.reshape(blocks_here, BLOCK, width_here)
    edge_slots = 0
    owner_flat = random_owner.reshape(-1)
    local_flat = random_local.reshape(-1)
    request_table, slot_ids = slot_table(owner_flat, local_flat, seq_count, slot_count)
    wanted = lax.all_to_all(request_table, "seq", split_axis=0, concat_axis=0, tiled=True)
    sent_keys = jnp.take(key_blocks, wanted, axis=0)
    sent_values = jnp.take(value_blocks, wanted, axis=0)
    got_keys = lax.all_to_all(sent_keys, "seq", split_axis=0, concat_axis=0, tiled=True)
    got_values = lax.all_to_all(sent_values, "seq", split_axis=0, concat_axis=0, tiled=True)
    slot_width = slot_count + edge_slots
    flat_slots = owner_flat * slot_width + slot_ids
    random_keys = jnp.take(got_keys.reshape(-1, BLOCK, width_here), flat_slots, axis=0)
    random_values = jnp.take(got_values.reshape(-1, BLOCK, width_here), flat_slots, axis=0)
    edge_pairs = jnp.stack(
        [jnp.stack([key_blocks[0], value_blocks[0]]), jnp.stack([key_blocks[-1], value_blocks[-1]])]
    )
    widened = padded(edge_pairs, (("seq", 0),), 1)
    left_key, left_value = (widened[0, 0], widened[0, 1])
    right_key, right_value = (widened[3, 0], widened[3, 1])
    global_rows = jnp.stack([queries[:GLOBAL], key_rows[:GLOBAL], value_rows[:GLOBAL]])
    global_rows = from_root(global_rows, "seq", 0)
    global_query = global_rows[0].reshape(GLOBAL, heads_here, HEAD_DIM)
    key_heads = key_rows.reshape(token_count, heads_here, HEAD_DIM)
    value_heads = value_rows.reshape(token_count, heads_here, HEAD_DIM)
    scores = (
        jnp.einsum("qhd,khd->hqk", global_query, key_heads, preferred_element_type=jnp.float32)
        * score_scale
    )
    row_max = jnp.max(scores, axis=2)
    weight = jnp.exp(scores - row_max[:, :, None])
    row_total = jnp.sum(weight, axis=2)
    partial_value = jnp.einsum(
        "hqk,khd->hqd", weight.astype(jnp.bfloat16), value_heads, preferred_element_type=jnp.float32
    )

    def combine(left_part, right_part):
        joint_max = jnp.maximum(left_part[0], right_part[0])
        left_factor = jnp.exp(left_part[0] - joint_max)
        right_factor = jnp.exp(right_part[0] - joint_max)
        return (
            joint_max,
            left_part[1] * left_factor + right_part[1] * right_factor,
            left_part[2] * left_factor[:, :, None] + right_part[2] * right_factor[:, :, None],
        )

    row_max, row_total, partial_value = combined_all(
        (row_max, row_total, partial_value), "seq", combine
    )
    global_out = jnp.transpose(partial_value / row_total[:, :, None], (1, 0, 2)).reshape(
        GLOBAL, width_here
    )
    key_padded = jnp.concatenate([left_key[None], key_blocks, right_key[None]], axis=0)
    value_padded = jnp.concatenate([left_value[None], value_blocks, right_value[None]], axis=0)
    global_keys = global_rows[1].reshape(GLOBAL // BLOCK, BLOCK, width_here)
    global_values = global_rows[2].reshape(GLOBAL // BLOCK, BLOCK, width_here)
    group_size = math.gcd(blocks_here, max(1, 512 // BLOCK))
    group_count = blocks_here // group_size
    listed = (3 + RANDOM) * BLOCK + GLOBAL
    slot_number = jnp.arange(listed, dtype=jnp.int32) // BLOCK

    def attend(packed):
        number, query_group, key_group, value_group = packed
        block_ids = (
            seq_index * blocks_here + number * group_size + jnp.arange(group_size, dtype=jnp.int32)
        )
        near_keys = lax.dynamic_slice_in_dim(key_padded, number * group_size, group_size + 2, 0)
        near_values = lax.dynamic_slice_in_dim(value_padded, number * group_size, group_size + 2, 0)
        window_keys = jnp.stack([near_keys[:-2], near_keys[1:-1], near_keys[2:]], axis=1)
        window_values = jnp.stack([near_values[:-2], near_values[1:-1], near_values[2:]], axis=1)
        listed_keys = jnp.concatenate(
            [
                window_keys,
                key_group,
                jnp.broadcast_to(global_keys[None], (group_size,) + global_keys.shape),
            ],
            axis=1,
        )
        listed_values = jnp.concatenate(
            [
                window_values,
                value_group,
                jnp.broadcast_to(global_values[None], (group_size,) + global_values.shape),
            ],
            axis=1,
        )
        group_keys = listed_keys.reshape(group_size, listed, heads_here, HEAD_DIM)
        group_values = listed_values.reshape(group_size, listed, heads_here, HEAD_DIM)
        query_heads = query_group.reshape(group_size, BLOCK, heads_here, HEAD_DIM)
        block_scores = (
            jnp.einsum(
                "bqhd,bkhd->bhqk", query_heads, group_keys, preferred_element_type=jnp.float32
            )
            * score_scale
        )
        usable = jnp.logical_and(
            jnp.logical_or(slot_number[None, :] != 0, block_ids[:, None] > 0),
            jnp.logical_or(slot_number[None, :] != 2, block_ids[:, None] < total_blocks - 1),
        )
        usable_keys = usable[:, None, None, :]
        block_scores = jnp.where(usable_keys, block_scores, masked_score)
        block_max = jnp.max(block_scores, axis=3, keepdims=True)
        block_weight = jnp.where(usable_keys, jnp.exp(block_scores - block_max), 0.0)
        block_total = jnp.sum(block_weight, axis=3)
        context = jnp.einsum(
            "bhqk,bkhd->bqhd",
            block_weight.astype(jnp.bfloat16),
            group_values,
            preferred_element_type=jnp.float32,
        )
        context = context / jnp.transpose(block_total, (0, 2, 1))[:, :, :, None]
        return context.reshape(group_size * BLOCK, width_here).astype(jnp.bfloat16)

    numbers = jnp.arange(group_count, dtype=jnp.int32)
    query_groups = queries.reshape(group_count, group_size, BLOCK, width_here)
    random_key_groups = random_keys.reshape(group_count, group_size, RANDOM, BLOCK, width_here)
    random_value_groups = random_values.reshape(group_count, group_size, RANDOM, BLOCK, width_here)
    sparse = lax.map(
        attend, (numbers, query_groups, random_key_groups, random_value_groups)
    ).reshape(token_count, width_here)
    top_rows = jnp.where(seq_index == 0, global_out.astype(jnp.bfloat16), sparse[:GLOBAL])
    attention = jnp.concatenate([top_rows, sparse[GLOBAL:]], axis=0)
    summed = lax.psum_scatter(
        jnp.dot(attention, output_weight, preferred_element_type=jnp.float32),
        "head",
        scatter_dimension=0,
        tiled=True,
    )
    return summed.astype(jnp.bfloat16)


def solution(mesh):
    in_specs = (
        P("seq", "head"),
        P("seq", "head"),
        P("seq", "head"),
        P("seq", None),
        P("seq", None),
        P("head", None),
    )
    out_specs = P(("seq", "head"), None)
    return jax.shard_map(local, mesh=mesh, in_specs=in_specs, out_specs=out_specs, check_vma=False)
```

profile of v0, /device:TPU:0, one launch (start us, length us, event | category | flops | bytes accessed | tf_op | source)
XLA Modules:
  0.0 904.6 jit_solution(16662353208190921498)
XLA Ops:
  8.9 13.6 %all_to_all.22 = s32[8,1,8]{2,1,0:T(1,128)S(1)} all-to-all(s32[8,1,8]{2,1,0:T(1,128)S(1)} %bitcast.212), channel_id=1, replica_groups=mesh['seq'=8,'head'=4] {'seq'}, dimensions={0} | all-to-all | bytes 512 | tf_op jit(solution)/shard_map/all_to_all | solution.py:75
  22.6 7.1 gather_fusion
  29.7 5.4 gather_fusion.2
  35.1 9.4 %broadcast_select_fusion = (bf16[8,8,64,1024]{3,2,1,0:T(8,128)(2,1)}, bf16[8,8,64,1024]{3,2,1,0:T(8,128)(2,1)S(1)}) fusion(bf16[8,8,64,1024]{3,2,1,0:T(8,128)(2,1)} %bitcast.198, pred[8,8]{1,0:T(8,128)(4,1)S(1)} %compare_and_fusion, bf16[8,8,64,1024]{3,2,1,0:T(8,128)(2,1)} %bitcast.197), kind=kLoop, calls=%fused_computation.61 | loop fusion | flops 8388608 | bytes 33554496 | tf_op jit(solution)/shard_map/jit(_take)/select_n | solution.py:76
  44.5 185.8 %all_to_all.23 = bf16[8,8,64,1024]{3,2,1,0:T(8,128)(2,1)} all-to-all(bf16[8,8,64,1024]{3,2,1,0:T(8,128)(2,1)S(1)} %get-tuple-element.475), channel_id=1, replica_groups=mesh['seq'=8,'head'=4] {'seq'}, dimensions={0} | all-to-all | bytes 16777216 | tf_op jit(solution)/shard_map/all_to_all | solution.py:79
  230.3 5.2 all-to-all-start.2
  238.1 228.5 %all-reduce.2.cloned.1.call-done = bf16[3,128,1024]{1,2,0:T(8,128)(2,1)} async-done(((bf16[3,128,1024]{1,2,0:T(8,128)(2,1)}), bf16[3,128,1024]{1,2,0:T(8,128)(2,1)}) %all-reduce.2.cloned.1.call-update) | async-done | bytes 786448 | tf_op jit(solution)/shard_map/psum | solution.py:32
  468.8 1.9 copy-done.3
  470.7 2.1 fusion.38
  473.9 2.6 collective-permute-start
  477.9 11.4 %collective-permute-done = bf16[1,2,64,1024]{3,2,1,0:T(8,128)(2,1)S(1)} collective-permute-done((bf16[1,2,64,1024]{3,2,1,0:T(8,128)(2,1)S(1)}, bf16[1,2,64,1024]{3,2,1,0:T(8,128)(2,1)S(1)}, u32[]{:S(2)}, u32[]{:S(2)}) %collective-permute-start) | collective-permute-done | bytes 262176 | tf_op jit(solution)/shard_map/ppermute | solution.py:24
  490.2 1.9 pad_maximum_fusion
  492.1 1.7 pad_maximum_fusion.1
  494.7 33.3 %all-gather.1 = f32[64,128]{1,0:T(8,128)S(1)} all-gather(f32[8,128]{1,0:T(8,128)S(1)} %fusion.37), channel_id=3, replica_groups=mesh['seq'=8,'head'=4] {'seq'}, dimensions={0}, use_global_device_ids=true | all-gather | bytes 36864 | tf_op jit(solution)/shard_map/all_gather | solution.py:36
  528.0 31.3 %all-gather = f32[64,128]{1,0:T(8,128)S(1)} all-gather(f32[8,128]{1,0:T(8,128)S(1)} %get-tuple-element.480), channel_id=2, replica_groups=mesh['seq'=8,'head'=4] {'seq'}, dimensions={0}, use_global_device_ids=true | all-gather | bytes 36864 | tf_op jit(solution)/shard_map/all_gather | solution.py:36
  562.1 11.0 %while.33 = (s32[]{:T(128)}, f32[8,128]{1,0:T(8,128)S(1)}, f32[8,128]{1,0:T(8,128)S(1)}, f32[8,128,128]{2,1,0:T(8,128)S(1)}, f32[8,8,128]{2,1,0:T(8,128)S(1)}, /...) while((s32[]{:T(128)}, f32[8,128]{1,0:T(8,128)S(1)}, ...), condition=%wide.region_4.5_spmd, body=%wide.region_3.4_spmd.sunk | while | flops 399365 | bytes 1613975 | solution.py:42
  574.0 8.4 gather_fusion.1
  582.4 8.4 gather_fusion.3
  590.8 10.4 %broadcast_select_fusion.2 = (bf16[48,64,1024]{2,1,0:T(8,128)(2,1)}, bf16[48,64,1024]{2,1,0:T(8,128)(2,1)}) fusion(bf16[48,64,1024]{2,1,0:T(8,128)(2,1)} %gather_fusion.3, pred[48]{0:T(512)(128)(4,1)S(1)} %get-tuple-element.453, bf16[48,64,1024]{2,1,0:T(8,128)(2,1)} %gather_fusion.1), kind=kLoop, calls=%fused_computation.63 | loop fusion | flops 6291456 | bytes 25165872 | tf_op jit(solution)/shard_map/jit(_take)/select_n | solution.py:82
  601.2 146.4 %while.34 = (s32[]{:T(128)}, bf16[2,512,1024]{2,1,0:T(8,128)(2,1)}, s32[2]{0:T(128)S(1)}, bf16[18,64,1024]{2,1,0:T(8,128)(2,1)S(1)}, bf16[2,8,3,64,1024]{4,3,2,1...) while((s32[]{:T(128)}, bf16[2,512,1024]{2,1,0:T(8,128)(2,1)}, ...), condition=%wide.region_11.14_spmd.clone.clone, body=%wide.region_8.13_spmd.clone.clone.sunk | while | flops 1091585536 | bytes 126397792 | solution.py:187
  605.7 2.3 fusion.87
  607.9 2.3 fusion.88
  610.2 2.2 fusion.89
  612.4 6.7 bitcast_dynamic-update-slice_fusion.3
  619.1 2.5 broadcast_dynamic-update-slice_fusion.5
  621.6 8.9 copy.127
  630.9 9.6 %fusion.93 = f32[8,8,64,512]{3,2,1,0:T(8,128)} fusion(bf16[8,512,8,128]{3,2,1,0:T(8,128)(2,1)} %bitcast.186, bf16[8,64,8,128]{3,2,1,0:T(8,128)(2,1)S(1)} %bitcast.189), kind=kOutput, calls=%fused_computation.16.clone.1 | convolution fusion | flops 536870912 | bytes 17825792 | tf_op jit(solution)/shard_map/while/body/eval_jaxpr/bqhd,bkhd->bhqk/dot_general | solution.py:160
  640.7 11.5 %fusion.96 = (f32[8,8,64]{2,1,0:T(8,128)S(1)}, bf16[8,8,64,512]{3,2,1,0:T(8,128)(2,1)}) fusion(f32[8,8,64,512]{3,2,1,0:T(8,128)} %fusion.93, pred[8,512]{1,0:T(8,128)(4,1)S(1)} %or_and_fusion.2), kind=kOutput, calls=%fused_computation.111.clone.1 | output fusion | flops 16777728 | bytes 12603392 | tf_op jit(solution)/shard_map/while/body/eval_jaxpr/sub | solution.py:172
  652.2 2.5 broadcast_dynamic-update-slice_fusion.4
  654.7 8.8 copy.126
  663.4 6.6 fusion.97
  670.1 1.7 copy.129
  678.8 2.3 fusion.87
  681.1 2.3 fusion.88
  683.4 2.2 fusion.89
  685.6 6.7 bitcast_dynamic-update-slice_fusion.3
  692.3 2.5 broadcast_dynamic-update-slice_fusion.5
  694.8 8.9 copy.127
  704.1 9.6 %fusion.93 = f32[8,8,64,512]{3,2,1,0:T(8,128)} fusion(bf16[8,512,8,128]{3,2,1,0:T(8,128)(2,1)} %bitcast.186, bf16[8,64,8,128]{3,2,1,0:T(8,128)(2,1)S(1)} %bitcast.189), kind=kOutput, calls=%fused_computation.16.clone.1 | convolution fusion | flops 536870912 | bytes 17825792 | tf_op jit(solution)/shard_map/while/body/eval_jaxpr/bqhd,bkhd->bhqk/dot_general | solution.py:160
  713.9 11.5 %fusion.96 = (f32[8,8,64]{2,1,0:T(8,128)S(1)}, bf16[8,8,64,512]{3,2,1,0:T(8,128)(2,1)}) fusion(f32[8,8,64,512]{3,2,1,0:T(8,128)} %fusion.93, pred[8,512]{1,0:T(8,128)(4,1)S(1)} %or_and_fusion.2), kind=kOutput, calls=%fused_computation.111.clone.1 | output fusion | flops 16777728 | bytes 12603392 | tf_op jit(solution)/shard_map/while/body/eval_jaxpr/sub | solution.py:172
  725.3 2.5 broadcast_dynamic-update-slice_fusion.4
  727.9 8.8 copy.126
  736.6 6.6 fusion.97
  743.3 1.7 copy.129
  750.4 2.5 copy.92
  752.9 16.1 %fusion.45 = f32[1024,4096]{1,0:T(8,128)} fusion(bf16[1024,4096]{1,0:T(8,128)(2,1)} %param.19, bf16[896,1024]{0,1:T(8,128)(2,1)} %copy.92, bf16[128,1024]{0,1:T(8,128)(2,1)S(1)} %bitcast_select_fusion), kind=kOutput, calls=%fused_computation.77 | convolution fusion | flops 8594128896 | bytes 27262976 | tf_op jit(solution)/shard_map/dot_general | solution.py:193
  769.0 125.2 %reduce-scatter.2.cloned.1.call-done = f32[256,4096]{1,0:T(8,128)} async-done(((f32[1024,4096]{1,0:T(8,128)}), f32[256,4096]{1,0:T(8,128)}) %reduce-scatter.2.cloned.1.call-update) | async-done | bytes 4194320 | tf_op jit(solution)/shard_map/reduce_scatter | solution.py:192
  894.3 3.8 convert_element_type.51
  (107 shorter events, 42.6 us)
Async XLA Ops:
  22.5 7.2 copy-start
  230.3 6.2 slice-start
  230.3 352.1 %all-to-all-start.2 = ((bf16[8,8,64,1024]{3,2,1,0:T(8,128)(2,1)}), bf16[8,8,64,1024]{3,2,1,0:T(8,128)(2,1)}, u32[]{:S(2)}, u32[]{:S(2)}) async-start(bf16[8,8,64,1024]{3,2,1,0:T(8,128)(2,1)} %get-tuple-element.474), calls=%async_computation.2 | async-start | bytes 16777216 | tf_op jit(solution)/shard_map/all_to_all | solution.py:78
  235.4 231.1 %all-reduce.2.cloned.1.call-start = ((), (), s32[]{:S(2)}) async-start(), calls=%async_computation.4 | async-start | bytes 1572864 | tf_op jit(solution)/shard_map/psum | solution.py:32
  238.1 322.9 %all-gather.5.cloned.1.call-start = ((), (), s32[]{:S(2)}) async-start(), calls=%async_computation.6 | async-start | bytes 4718592 | tf_op jit(solution)/shard_map/all_gather | solution.py:36
  466.6 4.1 copy-start.2
  468.8 1.9 copy-start.3
  472.8 421.5 %reduce-scatter.2.cloned.1.call-start = ((), (), s32[]{:S(2)}) async-start(), calls=%async_computation.5 | async-start | bytes 20971520 | tf_op jit(solution)/shard_map/reduce_scatter | solution.py:192
  473.9 15.4 %collective-permute-start = (bf16[1,2,64,1024]{3,2,1,0:T(8,128)(2,1)S(1)}, bf16[1,2,64,1024]{3,2,1,0:T(8,128)(2,1)S(1)}, u32[]{:S(2)}, u32[]{:S(2)}) collective-permute-start(bf16[1,2,64,1024]{3,2,1,0:T(8,128)(2,1)S(1)} %maximum_bitcast_fusion), channel_id=1, source_target_pairs={{0,4},{4,8},{8,12},{12,16},{16,20},{20,24},{24,28},{1,5},{5,9},{9,... | collective-permute-start | bytes 786440 | tf_op jit(solution)/shard_map/ppermute | solution.py:24
  476.5 13.6 %collective-permute-start.1 = (bf16[1,2,64,1024]{3,2,1,0:T(8,128)(2,1)S(1)}, bf16[1,2,64,1024]{3,2,1,0:T(8,128)(2,1)S(1)}, u32[]{:S(2)}, u32[]{:S(2)}) collective-permute-start(bf16[1,2,64,1024]{3,2,1,0:T(8,128)(2,1)S(1)} %maximum_bitcast_fusion.1), channel_id=1, source_target_pairs={{4,0},{8,4},{12,8},{16,12},{20,16},{24,20},{28,24},{5,1},{9,5},{13... | collective-permute-start | bytes 786440 | tf_op jit(solution)/shard_map/ppermute | solution.py:25
  477.9 14.2 %copy-start.1 = (bf16[1024,1024]{1,0:T(8,128)(2,1)S(1)}, bf16[1024,1024]{1,0:T(8,128)(2,1)}, u32[]{:S(2)}) copy-start(bf16[1024,1024]{1,0:T(8,128)(2,1)} %param.15) | copy-start | bytes 6291460
  477.9 15.9 %copy-start.4 = (f32[8,128,1024]{2,1,0:T(8,128)S(1)}, f32[8,128,1024]{2,1,0:T(8,128)}, u32[]{:S(2)}) copy-start(f32[8,128,1024]{2,1,0:T(8,128)} %copy-done.3) | copy-start | bytes 12582916
  621.6 8.9 copy-start.5
  694.8 8.9 copy-start.5
  747.5 5.3 copy-start.6
Sparse Core Ops, SparseCore 0:
  239.7 226.8 all-reduce.1
  472.9 75.0 all-gather.4
  769.2 125.0 reduce-scatter.1
where the time goes:
time: 906 us; the launch traced here: 905 us
  waiting for transfers between devices  366 us (40%)
  blocking collectives  264 us (29%)
  local copies, waits for them, and re-layouts  135 us (15%)
  other arithmetic  64.4 us (7%)
  matrix products  51.6 us (6%)
  between operations  13.4 us (1%)
  starting transfers between devices  9.2 us (1%)
    psum x1, waiting for transfers between devices, from_root(): return lax.psum(block, axis)  228 us
    all_to_all x1, blocking collectives, local(): lax.all_to_all(sent_values, 'seq', split_axis=0, concat_axis=0, tiled=True)  186 us
    reduce_scatter x1, waiting for transfers between devices, local(): lax.psum_scatter(jnp.dot(attention, output_weight, preferred_element_type...  125 us
    while x24, local copies, waits for them, and re-layouts  69.2 us
    all_gather x2, blocking collectives, combined_all(): everything = jax.tree.map(lambda part: lax.all_gather(part, axis), array)  64.6 us
    sub x2, other arithmetic, attend(): block_scores - block_max  23 us
    dot_general x2, matrix products, attend(): jnp.einsum('bqhd,bkhd->bhqk', query_heads, group_keys, preferred_element_...  19.3 us
  transfers between devices with their start and end apart: 6, of which 4 were waited for; matrix products, arithmetic and copies ran while one was open for 4% of the time, Pallas kernels for 0%

commit v1 on v0

--- a/solution.py
+++ b/solution.py
@@ -3,6 +3,8 @@
 import jax
 import jax.numpy as jnp
 from jax import lax
+from jax.experimental import pallas as pl
+from jax.experimental.pallas import tpu as pltpu
 from jax.sharding import PartitionSpec as P
 
 HEAD_DIM = 128
@@ -57,7 +59,7 @@
     return (request_table, slot_ids)
 
 
-def local(queries, key_rows, value_rows, random_owner, random_local, output_weight):
+def local_exchange(queries, key_rows, value_rows, random_owner, random_local, output_weight):
     seq_count = lax.axis_size("seq")
     seq_index = lax.axis_index("seq")
     token_count, width_here = queries.shape
@@ -198,6 +200,442 @@
     return summed.astype(jnp.bfloat16)
 
 
+LOG2E = 1.4426950408889634
+LAYERS = 4
+CHUNKS = (3, 4, 1)
+LANES = 128
+PIECE = 16
+GROUP = 4
+NEAR_GROUP = 8
+
+
+CONTRACT_LAST = (((1,), (1,)), ((), ()))
+CONTRACT_MID = (((1,), (0,)), ((), ()))
+FACTOR = HEAD_DIM ** (-0.5) * LOG2E
+
+
+def soft(queries, keys, values, biases=None):
+    scores = [
+        lax.dot_general(q, k, CONTRACT_LAST, preferred_element_type=jnp.float32)
+        for q, k in zip(queries, keys)
+    ]
+    if biases is not None:
+        scores = [score + bias for score, bias in zip(scores, biases)]
+    tops = [jnp.max(score, axis=1, keepdims=True) for score in scores]
+    weights = [jnp.exp2((score - top) * FACTOR) for score, top in zip(scores, tops)]
+    totals = [jnp.sum(weight, axis=1, keepdims=True) for weight in weights]
+    contexts = [
+        lax.dot_general(w.astype(jnp.bfloat16), v, CONTRACT_MID, preferred_element_type=jnp.float32)
+        for w, v in zip(weights, values)
+    ]
+    return list(zip(tops, totals, contexts))
+
+
+def aligned(start, size=BLOCK):
+    return pl.ds(pl.multiple_of(start, BLOCK), size)
+
+
+def keep(stats, rows, count, step, top, total):
+    lane = lax.broadcasted_iota(jnp.int32, (count, LANES), 1)
+    both = jnp.where(lane < 3 * PIECE, top, total)
+    stats[rows, :] = jnp.where(lane % PIECE == step, both, stats[rows, :])
+
+
+def pieces(value, heads):
+    lane = lax.broadcasted_iota(jnp.int32, value.shape, 1)
+    high = value.astype(jnp.bfloat16).astype(jnp.float32)
+    middle = (value - high).astype(jnp.bfloat16).astype(jnp.float32)
+    turn = lane // PIECE % 3
+    part = jnp.where(turn == 0, high, jnp.where(turn == 1, middle, value - high - middle))
+    used = jnp.logical_and(lane % PIECE < heads, lane < 6 * PIECE)
+    return jnp.where(used, part, 0.0).astype(jnp.bfloat16)
+
+
+def unpieced(value, head):
+    row = lax.broadcasted_iota(jnp.int32, (LANES, LANES), 0)
+    mine = row % PIECE == head
+    return [
+        jnp.dot(
+            value,
+            jnp.where(jnp.logical_and(mine, row // (3 * PIECE) == side), 1.0, 0.0).astype(jnp.bfloat16),
+            preferred_element_type=jnp.float32,
+        )
+        for side in range(2)
+    ]
+
+
+def near_attention(params, queries, key_rows, value_rows, before, after, tokens, total_blocks):
+    token_count, width = queries.shape
+    heads = width // HEAD_DIM
+    blocks_here = token_count // BLOCK
+    window = 3 * BLOCK
+
+    def body(par, query_ref, key_ref, value_ref, before_ref, after_ref, token_ref, out_ref, piece_ref, wide, stats):
+        step = pl.program_id(0)
+        for side, ref in ((0, key_ref), (1, value_ref)):
+            wide[side, 0:BLOCK, :] = before_ref[side]
+            wide[side, BLOCK : BLOCK + token_count, :] = ref[...]
+            wide[side, BLOCK + token_count : 2 * BLOCK + token_count, :] = after_ref[side]
+        place = lax.broadcasted_iota(jnp.int32, (1, window + GLOBAL), 1) // BLOCK
+        seq_index = par[0]
+
+        def some_blocks(turn, _):
+            numbers = [turn * NEAR_GROUP + i for i in range(NEAR_GROUP)]
+            here = [aligned(number * BLOCK) for number in numbers]
+            near = [aligned(number * BLOCK, window) for number in numbers]
+            keys, values = (
+                [jnp.concatenate([wide[side, rows, :], token_ref[side]], axis=0) for rows in near]
+                for side in range(2)
+            )
+            blocks = [seq_index * blocks_here + number for number in numbers]
+            biases = [
+                jnp.where(
+                    jnp.logical_or(
+                        jnp.logical_and(place == 0, block == 0),
+                        jnp.logical_and(place == 2, block == total_blocks - 1),
+                    ),
+                    masked_score,
+                    0.0,
+                )
+                for block in blocks
+            ]
+            found = soft([query_ref[rows, :] for rows in here], keys, values, biases)
+            for rows, block, (top, total, context) in zip(here, blocks, found):
+                out_ref[rows, :] = context
+                top = jnp.where(block < GLOBAL // BLOCK, masked_score, top)
+                keep(stats, rows, BLOCK, step, top, total)
+            return 0
+
+        lax.fori_loop(0, blocks_here // NEAR_GROUP, some_blocks, 0)
+
+        @pl.when(step == heads - 1)
+        def _():
+            piece_ref[...] = pieces(stats[...], heads)
+
+    column = pl.BlockSpec((token_count, HEAD_DIM), lambda h, par: (0, h))
+    edge = pl.BlockSpec((2, BLOCK, HEAD_DIM), lambda h, par: (0, 0, h))
+    return pl.pallas_call(
+        body,
+        grid_spec=pltpu.PrefetchScalarGridSpec(
+            num_scalar_prefetch=1,
+            grid=(heads,),
+            in_specs=[column, column, column, edge, edge, pl.BlockSpec((2, GLOBAL, HEAD_DIM), lambda h, par: (0, 0, h))],
+            out_specs=[column, pl.BlockSpec((token_count, LANES), lambda h, par: (0, 0))],
+            scratch_shapes=[
+                pltpu.VMEM((2, token_count + 2 * BLOCK, HEAD_DIM), jnp.bfloat16),
+                pltpu.VMEM((token_count, LANES), jnp.float32),
+            ],
+        ),
+        out_shape=[
+            jax.ShapeDtypeStruct((token_count, width), jnp.float32),
+            jax.ShapeDtypeStruct((token_count, LANES), jnp.bfloat16),
+        ],
+        compiler_params=pltpu.CompilerParams(dimension_semantics=("arbitrary",)),
+        cost_estimate=pl.CostEstimate(
+            flops=4 * width * token_count * (window + GLOBAL), bytes_accessed=8 * token_count * width, transcendentals=0
+        ),
+        name="near",
+    )(params, queries, key_rows, value_rows, before, after, tokens)
+
+
+def column_attention(params, queries, pairs, names):
+    width = queries[0].shape[1]
+    token_count = pairs[0].shape[1]
+    heads = width // HEAD_DIM
+    blocks_here = token_count // BLOCK
+    column_tokens = len(pairs) * token_count
+    asked = RANDOM * BLOCK
+    callers = len(queries)
+
+    def body(par, *rest):
+        query_refs = rest[:callers]
+        pair_refs = rest[callers : callers + len(pairs)]
+        outs = rest[callers + len(pairs) : 2 * callers + len(pairs)]
+        buf, stats, sems = rest[2 * callers + len(pairs) :]
+        step = pl.program_id(0)
+        slot = lax.rem(step, 2)
+
+        def copies(head, into):
+            columns = pl.ds(pl.multiple_of(head * HEAD_DIM, HEAD_DIM), HEAD_DIM)
+            return [
+                pltpu.make_async_copy(
+                    ref.at[:, :, columns],
+                    buf.at[into, :, aligned(par[names["layer"] + number] * token_count, token_count), :],
+                    sems.at[into, number],
+                )
+                for number, ref in enumerate(pair_refs)
+            ]
+
+        def work():
+            @pl.when(step == 0)
+            def _():
+                for copy in copies(0, 0):
+                    copy.start()
+
+            @pl.when(step + 1 < heads)
+            def _():
+                for copy in copies(step + 1, 1 - slot):
+                    copy.start()
+
+            for copy in copies(step, slot):
+                copy.wait()
+
+            columns = pl.ds(pl.multiple_of(step * HEAD_DIM, HEAD_DIM), HEAD_DIM)
+            place = lax.broadcasted_iota(jnp.int32, (1, asked), 1) // BLOCK
+
+            def store(caller, rows, count, top, total, context):
+                outs[caller][rows, columns] = context.astype(jnp.bfloat16)
+                keep(stats.at[caller], rows, count, step, top, total)
+
+            def some_blocks(turn, _):
+                chosen = [(caller, turn * GROUP + i) for i in range(GROUP) for caller in range(callers)]
+                here = [aligned(number * BLOCK) for _, number in chosen]
+                places_of = [caller * blocks_here + number for caller, number in chosen]
+                spots = [
+                    [aligned(par[names["spots"] + at * RANDOM + r]) for r in range(RANDOM)] for at in places_of
+                ]
+                keys, values = (
+                    [jnp.concatenate([buf[slot, side, spot, :] for spot in row], axis=0) for row in spots]
+                    for side in range(2)
+                )
+                biases = [
+                    jnp.where(place < par[names["counts"] + at], 0.0, masked_score) for at in places_of
+                ]
+                asked_by = [query_refs[caller][rows, :] for (caller, _), rows in zip(chosen, here)]
+                found = soft(asked_by, keys, values, biases)
+                for (caller, _), rows, part in zip(chosen, here, found):
+                    store(caller, rows, BLOCK, *part)
+                return 0
+
+            lax.fori_loop(0, blocks_here // GROUP, some_blocks, 0)
+
+            for caller in range(callers):
+
+                @pl.when(par[names["device"] + caller] == 0)
+                def _():
+                    query = query_refs[caller][0:GLOBAL, :]
+                    rows = [slice(n * token_count, (n + 1) * token_count) for n in range(len(pairs))]
+                    keys, values = ([buf[slot, side, row, :] for row in rows] for side in range(2))
+                    found = soft([query] * len(pairs), keys, values)
+                    joint = found[0][0]
+                    for part in found[1:]:
+                        joint = jnp.maximum(joint, part[0])
+                    shares = [jnp.exp2((part[0] - joint) * FACTOR) for part in found]
+                    total = sum(part[1] * share for part, share in zip(found, shares))
+                    context = sum(part[2] * share for part, share in zip(found, shares))
+                    store(caller, slice(0, GLOBAL), GLOBAL, joint, total, context)
+
+                @pl.when(step == heads - 1)
+                def _():
+                    outs[caller][:, width:] = pieces(stats[caller], heads)
+
+        pl.when(par[names["inner"]] == 1)(work)
+
+    return pl.pallas_call(
+        body,
+        grid_spec=pltpu.PrefetchScalarGridSpec(
+            num_scalar_prefetch=1,
+            grid=(heads,),
+            in_specs=[pl.BlockSpec((token_count, HEAD_DIM), lambda h, par: (0, h))] * callers
+            + [pl.BlockSpec(memory_space=pl.ANY)] * len(pairs),
+            out_specs=[pl.BlockSpec((token_count, width + LANES), lambda h, par: (0, 0))] * callers,
+            scratch_shapes=[
+                pltpu.VMEM((2, 2, column_tokens, HEAD_DIM), jnp.bfloat16),
+                pltpu.VMEM((callers, token_count, LANES), jnp.float32),
+                pltpu.SemaphoreType.DMA((2, len(pairs))),
+            ],
+        ),
+        out_shape=[jax.ShapeDtypeStruct((token_count, width + LANES), jnp.bfloat16)] * callers,
+        compiler_params=pltpu.CompilerParams(dimension_semantics=("arbitrary",)),
+        cost_estimate=pl.CostEstimate(
+            flops=4 * width * token_count * callers * asked, bytes_accessed=4 * column_tokens * width, transcendentals=0
+        ),
+    )(params, *queries, *pairs)
+
+
+def merge(params, near, near_lse, inner_pair, outer_pair, first_head, names, head_count):
+    token_count = near.shape[0]
+    width = inner_pair[0].shape[1] - LANES
+    heads = width // HEAD_DIM
+    quarter = token_count // head_count
+    some = inner_pair + outer_pair
+
+    def body(par, near_ref, lse_ref, *rest):
+        parts = rest[: 2 * len(some)]
+        outs = rest[2 * len(some) : -1]
+        done = rest[-1]
+        step = pl.program_id(0)
+
+        def join(group):
+            found = [unpieced(lse_ref[...], first_head + step) + [near_ref[...]]]
+            for number in group:
+                context = parts[2 * number][...].astype(jnp.float32)
+                found.append(unpieced(parts[2 * number + 1][...], step) + [context])
+            top = jnp.maximum(jnp.maximum(found[0][0], found[1][0]), found[2][0])
+            shares = [jnp.exp2((part[0] - top) * FACTOR) for part in found]
+            total = sum(part[1] * share for part, share in zip(found, shares))
+            context = sum(part[2] * share for part, share in zip(found, shares))
+            done[...] = (context / total).astype(jnp.bfloat16)
+
+        pl.when(par[names["inner"]] == 1)(lambda: join((0, 1)))
+        pl.when(par[names["inner"]] == 0)(lambda: join((2, 3)))
+        for number in range(head_count):
+            start = jnp.bitwise_xor(par[names["head"]], number) * quarter
+            outs[number][...] = done[pl.ds(pl.multiple_of(start, quarter), quarter), :]
+
+    part_specs = [
+        pl.BlockSpec((token_count, HEAD_DIM), lambda h, par: (0, h)),
+        pl.BlockSpec((token_count, LANES), lambda h, par: (0, heads)),
+    ]
+    return pl.pallas_call(
+        body,
+        grid_spec=pltpu.PrefetchScalarGridSpec(
+            num_scalar_prefetch=1,
+            grid=(heads,),
+            in_specs=[
+                pl.BlockSpec((token_count, HEAD_DIM), lambda h, par: (0, first_head + h)),
+                pl.BlockSpec((token_count, LANES), lambda h, par: (0, 0)),
+            ]
+            + part_specs * len(some),
+            out_specs=[pl.BlockSpec((quarter, HEAD_DIM), lambda h, par: (0, h))] * head_count,
+            scratch_shapes=[pltpu.VMEM((token_count, HEAD_DIM), jnp.bfloat16)],
+        ),
+        out_shape=[jax.ShapeDtypeStruct((quarter, width), jnp.bfloat16)] * head_count,
+        compiler_params=pltpu.CompilerParams(dimension_semantics=("arbitrary",)),
+        cost_estimate=pl.CostEstimate(flops=64 * token_count * width, bytes_accessed=8 * token_count * width, transcendentals=0),
+    )(params, near, near_lse, *[part for part in some for _ in range(2)])
+
+
+def project(parts, weights, row_starts, tile=512):
+    rows = parts[0][0].shape[0]
+    depth, width = weights[0].shape
+    chunks = len(row_starts)
+
+    def body(*refs):
+        part_refs = refs[: len(weights) * chunks]
+        weight_refs = refs[len(weights) * chunks : -1]
+        total = jnp.zeros((rows, tile), jnp.float32)
+        for number, weight in enumerate(weight_refs):
+            left = jnp.concatenate(
+                [part_refs[number * chunks + c][...] for c in range(chunks)], axis=1
+            )
+            total = total + jnp.dot(left, weight[...], preferred_element_type=jnp.float32)
+        refs[-1][...] = total.astype(jnp.bfloat16)
+
+    flat = [part for group in parts for part in group]
+    return pl.pallas_call(
+        body,
+        grid=(width // tile,),
+        in_specs=[pl.BlockSpec(part.shape, lambda n: (0, 0)) for part in flat]
+        + [pl.BlockSpec((depth, tile), lambda n: (0, n))] * len(weights),
+        out_specs=pl.BlockSpec((rows, tile), lambda n: (0, n)),
+        out_shape=jax.ShapeDtypeStruct((rows, width), jnp.bfloat16),
+        compiler_params=pltpu.CompilerParams(dimension_semantics=("arbitrary",)),
+        cost_estimate=pl.CostEstimate(
+            flops=2 * rows * depth * len(weights) * width, bytes_accessed=2 * depth * len(weights) * width, transcendentals=0
+        ),
+        name="project",
+    )(*flat, *weights)
+
+
+def local_columns(queries, key_rows, value_rows, random_owner, random_local, output_weight):
+    seq_count, head_count = lax.axis_size("seq"), lax.axis_size("head")
+    token_count, width_here = queries.shape
+    heads_here = width_here // HEAD_DIM
+    blocks_here = token_count // BLOCK
+    seq_index, head_index = lax.axis_index("seq"), lax.axis_index("head")
+    layer, side = seq_index // 2, seq_index % 2
+    last = LAYERS - 1
+    inner = jnp.logical_and(layer > 0, layer < last)
+    outer_layer = jnp.where(layer * 2 < last, 0, last)
+    mirror = last - layer
+    ends = ((0, 1), (last, last - 1))
+    to_inner = [(2 * a + x, 2 * b + x) for a, b in ends for x in range(2)]
+    to_inner_across = [(2 * a + x, 2 * b + 1 - x) for a, b in ends for x in range(2)]
+    to_outer = [(b, a) for a, b in to_inner]
+    to_outer_across = [(b, a) for a, b in to_inner_across]
+    middle = [(2 * a + x, 2 * (last - a) + x) for _, a in ends for x in range(2)]
+    across = [(2 * a + x, 2 * a + 1 - x) for _, a in ends for x in range(2)]
+
+    def move(array, pairs):
+        return lax.ppermute(array, "seq", pairs)
+
+    def swap(array, distance):
+        return lax.ppermute(array, "head", [(i, i ^ distance) for i in range(head_count)])
+
+    last_block = jnp.stack([key_rows[-BLOCK:], value_rows[-BLOCK:]])
+    first_block = jnp.stack([key_rows[:BLOCK], value_rows[:BLOCK]])
+    before = move(last_block, [(i, i + 1) for i in range(seq_count - 1)])
+    after = move(first_block, [(i + 1, i) for i in range(seq_count - 1)])
+    tokens = jnp.stack([key_rows[:GLOBAL], value_rows[:GLOBAL]])
+    hops = [[(0, 1)]] + [[(2 * z + x, 2 * z + 2 + x) for x in range(2)] for z in range(LAYERS - 1)]
+    for pairs in hops:
+        got = move(tokens, pairs)
+        reached = jnp.any(jnp.array([b for _, b in pairs]) == seq_index)
+        tokens = jnp.where(reached, got, tokens)
+
+    far_weight = swap(output_weight, 2)
+    near, near_lse = near_attention(
+        seq_index.astype(jnp.int32).reshape(1), queries, key_rows, value_rows, before, after, tokens, seq_count * blocks_here
+    )
+
+    parts = [[] for _ in range(head_count)]
+    first_head = 0
+    moved = []
+    for number, size in enumerate(CHUNKS):
+        size = heads_here * size // sum(CHUNKS)
+        columns = slice(first_head * HEAD_DIM, (first_head + size) * HEAD_DIM)
+        pair = jnp.stack([key_rows[:, columns], value_rows[:, columns]])
+        query = queries[:, columns]
+        if number == 0:
+            listed = jnp.concatenate([random_owner, random_local], axis=1).astype(queries.dtype)
+            spare = (0, query.shape[1] - 2 * RANDOM)
+            query = jnp.concatenate([query, jnp.pad(listed, ((0, 0), spare))], axis=0)
+        outer_pair = move(pair, to_inner)
+        mirror_pair = move(pair, middle)
+        callers = [query, move(query, to_inner), move(query, across), move(query, to_inner_across)]
+        mirror_outer = move(outer_pair, middle)
+        moved.append((first_head, callers, [pair, outer_pair, mirror_pair, mirror_outer]))
+        first_head += size
+    tables = jnp.stack([asked[token_count:, : 2 * RANDOM] for asked in moved[0][1]]).astype(jnp.int32)
+    owners, locals_of = tables[:, :, :RANDOM], tables[:, :, RANDOM:]
+    spots = owners // 2 * token_count + locals_of * BLOCK
+    here = (owners % 2 == side).astype(jnp.int32)
+    rank = jnp.cumsum(here, axis=2) - 1
+    packed = [
+        jnp.sum(jnp.where(jnp.logical_and(here == 1, rank == r), spots, 0), axis=2) for r in range(RANDOM)
+    ]
+    outer_device = 2 * outer_layer + side
+    head_line = [seq_index, head_index, inner]
+    layers = [layer, outer_layer, mirror, last - outer_layer]
+    devices = [seq_index, outer_device, seq_index + 1 - 2 * side, outer_device + 1 - 2 * side]
+    params = jnp.concatenate(
+        [
+            jnp.stack([jnp.asarray(v, jnp.int32) for v in head_line + layers + devices]),
+            jnp.stack(packed, axis=2).reshape(-1),
+            jnp.sum(here, axis=2).reshape(-1),
+        ]
+    ).astype(jnp.int32)
+    names = {"seq": 0, "head": 1, "inner": 2, "layer": 3, "device": 7, "spots": 11}
+    names["counts"] = 11 + 4 * blocks_here * RANDOM
+
+    for first, callers, pairs in moved:
+        found = column_attention(params, callers, pairs, names)
+        inner_pair = [found[0], move(found[2], across)]
+        outer_pair = [move(found[1], to_outer), move(found[3], to_outer_across)]
+        outs = merge(params, near, near_lse, inner_pair, outer_pair, first, names, head_count)
+        for distance, part in enumerate(outs):
+            parts[distance].append(swap(part, distance) if distance else part)
+    weights = [output_weight, swap(output_weight, 1), far_weight, swap(far_weight, 1)]
+    return project(parts, weights, moved)
+
+
+def local(*arrays):
+    if lax.axis_size("seq") != 2 * LAYERS:
+        return local_exchange(*arrays)
+    return local_columns(*arrays)
+
+
 def solution(mesh):
     in_specs = (
         P("seq", "head"),

time: 906 us -> 554 us (0.61)
  blocking collectives: 264 us -> 0 us
  local copies, waits for them, and re-layouts: 135 us -> 13.7 us
  starting transfers between devices: 9.2 us -> 123 us
  Pallas kernels: 0 us -> 63.3 us
  other arithmetic: 64.4 us -> 12 us
  matrix products: 51.6 us -> 0 us
  waiting for transfers between devices: 366 us -> 339 us
  between operations: 13.4 us -> 0.72 us
    ppermute x2 -> x45, waiting for transfers between devices: 12.2 us -> 339 us  [the longest x33 252 us: move(): return lax.ppermute(array, 'seq', pairs)]
    psum x1 -> x0, waiting for transfers between devices: 228 us -> none  [from_root(): return lax.psum(block, axis)]
    all_to_all x2 -> x0, blocking collectives: 199 us -> none  [the longest x1 186 us: local(): lax.all_to_all(sent_values, 'seq', split_axis=0, concat_axis=0, tiled=True)]
    reduce_scatter x1 -> x0, waiting for transfers between devices: 125 us -> none  [local(): lax.psum_scatter(jnp.dot(attention, output_weight, preferred_element_type...]
    ppermute x2 -> x45, starting transfers between devices: 3.91 us -> 123 us  [the longest x33 112 us: move(): return lax.ppermute(array, 'seq', pairs)]
    while x25 -> x0, local copies, waits for them, and re-layouts: 69.4 us -> none
    all_gather x2 -> x0, blocking collectives: 64.6 us -> none  [combined_all(): everything = jax.tree.map(lambda part: lax.all_gather(part, axis), array)]
    pallas_call x0 -> x8, Pallas kernels: none -> 63.3 us  [the longest x3 18.8 us: merge(): pl.pallas_call(body, grid_spec=pltpu.PrefetchScalarGridSpec(num_scalar_pr...]
  transfers between devices with their start and end apart: 6 -> 45, of which waited for: 4 -> 12; matrix products, arithmetic and copies ran while one was open for 4% -> 4% of each run, Pallas kernels for 0% -> 8%
where the time goes in v1:
time: 554 us; the launch traced here: 552 us
  waiting for transfers between devices  339 us (61%)
  starting transfers between devices  123 us (22%)
  Pallas kernels  63.3 us (11%)
  local copies, waits for them, and re-layouts  13.7 us (2%)
  other arithmetic  12 us (2%)
    ppermute x33, waiting for transfers between devices, move(): return lax.ppermute(array, 'seq', pairs)  252 us
    ppermute x33, starting transfers between devices, move(): return lax.ppermute(array, 'seq', pairs)  112 us
    ppermute x12, waiting for transfers between devices, swap(): lax.ppermute(array, 'head', [(i, i ^ distance) for i in range(head_count)])  87.2 us
    pallas_call x3, Pallas kernels, merge(): pl.pallas_call(body, grid_spec=pltpu.PrefetchScalarGridSpec(num_scalar_pr...  18.8 us
    pallas_call x1, Pallas kernels, project(): pl.pallas_call(body, grid=(width // tile,), in_specs=[pl.BlockSpec(part.s...  17.6 us
    pallas_call x3, Pallas kernels, column_attention(): pl.pallas_call(body, grid_spec=pltpu.PrefetchScalarGridSpec(num_scalar_pr...  14.3 us
    pallas_call x1, Pallas kernels, near_attention(): pl.pallas_call(body, grid_spec=pltpu.PrefetchScalarGridSpec(num_scalar_pr...  12.6 us
    ppermute x12, starting transfers between devices, swap(): lax.ppermute(array, 'head', [(i, i ^ distance) for i in range(head_count)])  11.5 us
  transfers between devices with their start and end apart: 45, of which 12 were waited for; matrix products, arithmetic and copies ran while one was open for 4% of the time, Pallas kernels for 8%

profile of v1, /device:TPU:0, one launch (start us, length us, event | category | flops | bytes accessed | tf_op | source)
XLA Modules:
  0.0 552.2 jit_solution(15785518204637385578)
XLA Ops:
  0.0 3.0 collective-permute-start.43
  3.0 1.7 slice.78.rest_0_
  4.7 5.1 collective-permute-start.26
  11.1 2.4 collective-permute-start.24
  15.5 1.5 collective-permute-start.28
  21.7 2.4 collective-permute-start.3
  25.5 5.4 collective-permute-start.5
  31.8 3.9 collective-permute-done.3.before_ref
  35.8 4.1 collective-permute-start.2
  39.9 1.5 collective-permute-start.1
  41.5 18.5 %collective-permute-start = (bf16[1040,384]{1,0:T(8,128)(2,1)}, bf16[1040,384]{1,0:T(8,128)(2,1)}, u32[]{:S(2)}, u32[]{:S(2)}) collective-permute-start(bf16[1040,384]{1,0:T(8,128)(2,1)} %pad_maximum_fusion.2.rest_0_), channel_id=1, source_target_pairs={{0,8},{4,12},{24,16},{28,20},{1,9},{5,13},{25,17},{29,21},{2,10},{... | collective-permute-start | bytes 2396168 | tf_op jit(solution)/shard_map/ppermute | solution.py:561
  59.9 2.1 collective-permute-start.27
  64.2 1.8 broadcast_select_fusion
  66.0 21.9 %collective-permute-done.27.rest_5_ = bf16[2,1024,128]{2,1,0:T(8,128)(2,1)} collective-permute-done((bf16[2,1024,128]{2,1,0:T(8,128)(2,1)}, bf16[2,1024,128]{2,1,0:T(8,128)(2,1)}, u32[]{:S(2)}, u32[]{:S(2)}) %collective-permute-start.27) | collective-permute-done | bytes 524320 | tf_op jit(solution)/shard_map/ppermute | solution.py:561
  87.9 5.2 collective-permute-start.6
  93.0 1.5 collective-permute-start.29
  94.5 3.1 collective-permute-start.17
  97.7 1.6 collective-permute-start.16
  101.7 8.2 %collective-permute-start.15 = (bf16[1024,512]{1,0:T(8,128)(2,1)S(1)}, bf16[1024,512]{1,0:T(8,128)(2,1)}, u32[]{:S(2)}, u32[]{:S(2)}) collective-permute-start(bf16[1024,512]{1,0:T(8,128)(2,1)S(1)} %slice.75.rest_0_), channel_id=1, source_target_pairs={{0,8},{4,12},{24,16},{28,20},{1,9},{5,13},{25,17},{29,21},{2,10},{... | collective-permute-start | bytes 3145736 | tf_op jit(solution)/shard_map/ppermute | solution.py:561
  109.8 73.9 %collective-permute-done.43.refs_14_ = bf16[1024,4096]{1,0:T(8,128)(2,1)} collective-permute-done((bf16[1024,4096]{1,0:T(8,128)(2,1)}, bf16[1024,4096]{1,0:T(8,128)(2,1)}, u32[]{:S(2)}, u32[]{:S(2)}) %collective-permute-start.43) | collective-permute-done | bytes 8388640 | tf_op jit(solution)/shard_map/ppermute | solution.py:564
  184.9 3.3 shard_map.104
  188.2 1.8 broadcast_select_fusion.1
  191.9 1.4 collective-permute-start.31
  195.1 25.6 %collective-permute-start.18 = (bf16[2,1024,512]{2,1,0:T(8,128)(2,1)S(1)}, bf16[2,1024,512]{2,1,0:T(8,128)(2,1)}, u32[]{:S(2)}, u32[]{:S(2)}) collective-permute-start(bf16[2,1024,512]{2,1,0:T(8,128)(2,1)S(1)} %pad_maximum_fusion.rest_4_), channel_id=1, source_target_pairs={{0,8},{4,12},{24,16},{28,20},{1,9},{5,13},{25,17},{29,21},{2,10},{... | collective-permute-start | bytes 6291464 | tf_op jit(solution)/shard_map/ppermute | solution.py:561
  221.7 8.0 %collective-permute-done.32.rest_6_.rest_7_ = bf16[1024,256]{1,0:T(8,128)(2,1)S(1)} collective-permute-done((bf16[1024,256]{1,0:T(8,128)(2,1)S(1)}, bf16[1024,256]{1,0:T(8,128)(2,1)S(1)}, u32[]{:S(2)}, u32[]{:S(2)}) %collective-permute-start.32) | collective-permute-done | bytes 524320 | tf_op jit(solution)/shard_map/ppermute | solution.py:561
  229.7 2.6 collective-permute-start.9
  233.0 1.9 collective-permute-start.19
  235.7 61.8 %collective-permute-done.9.rest_5_ = bf16[2,1024,384]{2,1,0:T(8,128)(2,1)} collective-permute-done((bf16[2,1024,384]{2,1,0:T(8,128)(2,1)S(1)}, bf16[2,1024,384]{2,1,0:T(8,128)(2,1)}, u32[]{:S(2)}, u32[]{:S(2)}) %collective-permute-start.9) | collective-permute-done | bytes 1572896 | tf_op jit(solution)/shard_map/ppermute | solution.py:561
  298.2 2.0 collective-permute-start.20
  300.2 1.8 collective-permute-start.11
  302.7 1.5 broadcast_select_fusion.3.token_ref
  304.2 12.6 %near.1 = (f32[1024,1024]{1,0:T(8,128)}, bf16[1024,128]{1,0:T(8,128)(2,1)}) custom-call(s32[1]{0:T(128)} %bitcast.par, bf16[1024,1024]{1,0:T(8,128)(2,1)} %query_ref.1, bf16[1024,1024]{1,0:T(8,128)(2,1)} %key_ref.1, bf16[1024,1024]{1,0:T(8,128)(2,1)} %value_ref.1, bf16[2,64,1024]{2,1,0:T(8,128)(2,1)} %copy-done.19, bf16[2,64,1024]{2,1,0:T(8,128)(2,1)} %copy-done.20, ...), custom_call_target="tpu_custom_call" | custom-call | flops 1342177280 | bytes 8388608 | tf_op jit(solution)/shard_map/near/pallas_call | solution.py:317
  316.8 4.1 shard_map.105
  321.0 1.5 collective-permute-done.35.refs_5_
  322.4 1.5 collective-permute-start.38
  324.0 5.2 shard_map.100
  331.3 1.5 collective-permute-start.14
  332.8 5.9 %shard_map.102 = (bf16[1024,640]{1,0:T(8,128)(2,1)}, bf16[1024,640]{1,0:T(8,128)(2,1)}, bf16[1024,640]{1,0:T(8,128)(2,1)}, bf16[1024,640]{1,0:T(8,128)(2,1)}) custom-call(s32[267]{0:T(512)} %concatenate.29.par, bf16[1024,512]{1,0:T(8,128)(2,1)} %copy-done.6, bf16[1024,512]{1,0:T(8,128)(2,1)} %collective-permute-done.15.rest_1_, ...), custom_call_target="tpu_custom_call" | custom-call | flops 1610612736 | bytes 8388608 | tf_op jit(solution)/shard_map/pallas_call | solution.py:434
  340.4 91.6 %collective-permute-done.13.rest_4_.rest_5_ = bf16[1024,512]{1,0:T(8,128)(2,1)S(1)} collective-permute-done((bf16[1024,512]{1,0:T(8,128)(2,1)}, bf16[1024,512]{1,0:T(8,128)(2,1)S(1)}, u32[]{:S(2)}, u32[]{:S(2)}) %collective-permute-start.13) | collective-permute-done | bytes 1048608 | tf_op jit(solution)/shard_map/ppermute | solution.py:561
  434.3 20.2 %collective-permute-done.14.rest_6_.rest_7_ = bf16[1024,512]{1,0:T(8,128)(2,1)} collective-permute-done((bf16[1024,512]{1,0:T(8,128)(2,1)}, bf16[1024,512]{1,0:T(8,128)(2,1)}, u32[]{:S(2)}, u32[]{:S(2)}) %collective-permute-start.14) | collective-permute-done | bytes 1048608 | tf_op jit(solution)/shard_map/ppermute | solution.py:561
  455.8 6.8 %shard_map.101 = (bf16[256,384]{1,0:T(8,128)(2,1)}, bf16[256,384]{1,0:T(8,128)(2,1)}, bf16[256,384]{1,0:T(8,128)(2,1)}, bf16[256,384]{1,0:T(8,128)(2,1)}) custom-call(s32[267]{0:T(512)} %concatenate.29.par, f32[1024,1024]{1,0:T(8,128)} %get-tuple-element.31.near_ref, bf16[1024,128]{1,0:T(8,128)(2,1)} %get-tuple-element.32.lse_ref, ...), custom_call_target="tpu_custom_call" | custom-call | flops 25165824 | bytes 3145728 | tf_op jit(solution)/shard_map/pallas_call | solution.py:490
  463.9 18.7 %collective-permute-done.22.rest_4_.rest_5_ = bf16[1024,640]{1,0:T(8,128)(2,1)S(1)} collective-permute-done((bf16[1024,640]{1,0:T(8,128)(2,1)}, bf16[1024,640]{1,0:T(8,128)(2,1)S(1)}, u32[]{:S(2)}, u32[]{:S(2)}) %collective-permute-start.22) | collective-permute-done | bytes 1310752 | tf_op jit(solution)/shard_map/ppermute | solution.py:561
  482.6 2.2 collective-permute-start.36
  484.7 26.0 %collective-permute-done.23.rest_6_.rest_7_ = bf16[1024,640]{1,0:T(8,128)(2,1)} collective-permute-done((bf16[1024,640]{1,0:T(8,128)(2,1)}, bf16[1024,640]{1,0:T(8,128)(2,1)}, u32[]{:S(2)}, u32[]{:S(2)}) %collective-permute-start.23) | collective-permute-done | bytes 1310752 | tf_op jit(solution)/shard_map/ppermute | solution.py:561
  511.9 7.9 %shard_map.103 = (bf16[256,512]{1,0:T(8,128)(2,1)}, bf16[256,512]{1,0:T(8,128)(2,1)}, bf16[256,512]{1,0:T(8,128)(2,1)}, bf16[256,512]{1,0:T(8,128)(2,1)}) custom-call(s32[267]{0:T(512)} %concatenate.29.par, f32[1024,1024]{1,0:T(8,128)} %get-tuple-element.31.near_ref, bf16[1024,128]{1,0:T(8,128)(2,1)} %get-tuple-element.32.lse_ref, ...), custom_call_target="tpu_custom_call" | custom-call | flops 33554432 | bytes 4194304 | tf_op jit(solution)/shard_map/pallas_call | solution.py:490
  522.1 7.9 %collective-permute-done.37.refs_7_ = bf16[256,512]{1,0:T(8,128)(2,1)S(1)} collective-permute-done((bf16[256,512]{1,0:T(8,128)(2,1)}, bf16[256,512]{1,0:T(8,128)(2,1)S(1)}, u32[]{:S(2)}, u32[]{:S(2)}) %collective-permute-start.37) | collective-permute-done | bytes 262176 | tf_op jit(solution)/shard_map/ppermute | solution.py:564
  530.0 3.9 collective-permute-done.40.refs_10_
  534.6 17.6 %project.1 = bf16[256,4096]{1,0:T(8,128)(2,1)} custom-call(bf16[256,384]{1,0:T(8,128)(2,1)} %get-tuple-element.37.refs_0_, bf16[256,512]{1,0:T(8,128)(2,1)} %get-tuple-element.42.refs_1_, bf16[256,128]{1,0:T(8,128)(2,1)} %get-tuple-element.47.refs_2_, bf16[256,384]{1,0:T(8,128)(2,1)} %copy-done.21, bf16[256,512]{1,0:T(8,128)(2,1)} %copy-done.14, ...), custom_call_target="tpu_custom_call" | custom-call | flops 8589934592 | bytes 33554432 | tf_op jit(solution)/shard_map/project/pallas_call | solution.py:526
  (163 shorter events, 36.0 us)
Async XLA Ops:
  0.0 183.8 %collective-permute-start.43 = (bf16[1024,4096]{1,0:T(8,128)(2,1)}, bf16[1024,4096]{1,0:T(8,128)(2,1)}, u32[]{:S(2)}, u32[]{:S(2)}) collective-permute-start(bf16[1024,4096]{1,0:T(8,128)(2,1)} %refs_12_.1), channel_id=1, source_target_pairs={{0,2},{1,3},{2,0},{3,1},{4,6},{5,7},{6,4},{7,5},{8,10},{9,11},{10,... | collective-permute-start | bytes 25165832 | tf_op jit(solution)/shard_map/ppermute | solution.py:564
  4.7 16.2 %collective-permute-start.26 = (bf16[1024,128]{1,0:T(8,128)(2,1)}, bf16[1024,128]{1,0:T(8,128)(2,1)}, u32[]{:S(2)}, u32[]{:S(2)}) collective-permute-start(bf16[1024,128]{1,0:T(8,128)(2,1)} %slice.78.rest_0_), channel_id=1, source_target_pairs={{0,12},{4,8},{24,20},{28,16},{1,13},{5,9},{25,21},{29,17},{2,14},{... | collective-permute-start | bytes 786440 | tf_op jit(solution)/shard_map/ppermute | solution.py:561
  9.8 14.4 %collective-permute-start.25 = (bf16[1024,128]{1,0:T(8,128)(2,1)}, bf16[1024,128]{1,0:T(8,128)(2,1)}, u32[]{:S(2)}, u32[]{:S(2)}) collective-permute-start(bf16[1024,128]{1,0:T(8,128)(2,1)} %slice.78.rest_0_), channel_id=1, source_target_pairs={{8,12},{12,8},{16,20},{20,16},{9,13},{13,9},{17,21},{21,17},{10,14... | collective-permute-start | bytes 786440 | tf_op jit(solution)/shard_map/ppermute | solution.py:561
  11.1 14.4 %collective-permute-start.24 = (bf16[1024,128]{1,0:T(8,128)(2,1)}, bf16[1024,128]{1,0:T(8,128)(2,1)}, u32[]{:S(2)}, u32[]{:S(2)}) collective-permute-start(bf16[1024,128]{1,0:T(8,128)(2,1)} %slice.78.rest_0_), channel_id=1, source_target_pairs={{0,8},{4,12},{24,16},{28,20},{1,9},{5,13},{25,17},{29,21},{2,10},{... | collective-permute-start | bytes 786440 | tf_op jit(solution)/shard_map/ppermute | solution.py:561
  15.5 26.0 %collective-permute-start.28 = (bf16[2,1024,128]{2,1,0:T(8,128)(2,1)}, bf16[2,1024,128]{2,1,0:T(8,128)(2,1)}, u32[]{:S(2)}, u32[]{:S(2)}) collective-permute-start(bf16[2,1024,128]{2,1,0:T(8,128)(2,1)} %pad_maximum_fusion.4.rest_4_), channel_id=1, source_target_pairs={{8,16},{12,20},{16,8},{20,12},{9,17},{13,21},{17,9},{21,13},{10,18... | collective-permute-start | bytes 1572872 | tf_op jit(solution)/shard_map/ppermute | solution.py:561
  21.7 14.1 %collective-permute-start.3 = (bf16[2,64,1024]{2,1,0:T(8,128)(2,1)S(1)}, bf16[2,64,1024]{2,1,0:T(8,128)(2,1)S(1)}, u32[]{:S(2)}, u32[]{:S(2)}) collective-permute-start(bf16[2,64,1024]{2,1,0:T(8,128)(2,1)S(1)} %copy-done.18), channel_id=1, source_target_pairs={{0,4},{4,8},{8,12},{12,16},{16,20},{20,24},{24,28},{1,5},{5,9},{9,... | collective-permute-start | bytes 786440 | tf_op jit(solution)/shard_map/ppermute | solution.py:561
  24.2 15.7 %collective-permute-start.4 = (bf16[2,64,1024]{2,1,0:T(8,128)(2,1)S(1)}, bf16[2,64,1024]{2,1,0:T(8,128)(2,1)S(1)}, u32[]{:S(2)}, u32[]{:S(2)}) collective-permute-start(bf16[2,64,1024]{2,1,0:T(8,128)(2,1)S(1)} %copy-done.17), channel_id=1, source_target_pairs={{4,0},{8,4},{12,8},{16,12},{20,16},{24,20},{28,24},{5,1},{9,5},{13... | collective-permute-start | bytes 786440 | tf_op jit(solution)/shard_map/ppermute | solution.py:561
  25.5 34.4 %collective-permute-start.5 = (bf16[2,128,1024]{2,1,0:T(8,128)(2,1)S(1)}, bf16[2,128,1024]{2,1,0:T(8,128)(2,1)}, u32[]{:S(2)}, u32[]{:S(2)}) collective-permute-start(bf16[2,128,1024]{2,1,0:T(8,128)(2,1)S(1)} %pad_maximum_fusion.3), channel_id=1, source_target_pairs={{0,4},{1,5},{2,6},{3,7}} | collective-permute-start | bytes 1572872 | tf_op jit(solution)/shard_map/ppermute | solution.py:561
  35.8 57.3 %collective-permute-start.2 = (bf16[1040,384]{1,0:T(8,128)(2,1)}, bf16[1040,384]{1,0:T(8,128)(2,1)}, u32[]{:S(2)}, u32[]{:S(2)}) collective-permute-start(bf16[1040,384]{1,0:T(8,128)(2,1)} %pad_maximum_fusion.2.rest_0_), channel_id=1, source_target_pairs={{0,12},{4,8},{24,20},{28,16},{1,13},{5,9},{25,21},{29,17},{2,14},{... | collective-permute-start | bytes 2396168 | tf_op jit(solution)/shard_map/ppermute | solution.py:561
  39.9 54.6 %collective-permute-start.1 = (bf16[1040,384]{1,0:T(8,128)(2,1)}, bf16[1040,384]{1,0:T(8,128)(2,1)}, u32[]{:S(2)}, u32[]{:S(2)}) collective-permute-start(bf16[1040,384]{1,0:T(8,128)(2,1)} %pad_maximum_fusion.2.rest_0_), channel_id=1, source_target_pairs={{8,12},{12,8},{16,20},{20,16},{9,13},{13,9},{17,21},{21,17},{10,14... | collective-permute-start | bytes 2396168 | tf_op jit(solution)/shard_map/ppermute | solution.py:561
  41.5 56.2 %collective-permute-start = (bf16[1040,384]{1,0:T(8,128)(2,1)}, bf16[1040,384]{1,0:T(8,128)(2,1)}, u32[]{:S(2)}, u32[]{:S(2)}) collective-permute-start(bf16[1040,384]{1,0:T(8,128)(2,1)} %pad_maximum_fusion.2.rest_0_), channel_id=1, source_target_pairs={{0,8},{4,12},{24,16},{28,20},{1,9},{5,13},{25,17},{29,21},{2,10},{... | collective-permute-start | bytes 2396168 | tf_op jit(solution)/shard_map/ppermute | solution.py:561
  59.9 27.9 %collective-permute-start.27 = (bf16[2,1024,128]{2,1,0:T(8,128)(2,1)}, bf16[2,1024,128]{2,1,0:T(8,128)(2,1)}, u32[]{:S(2)}, u32[]{:S(2)}) collective-permute-start(bf16[2,1024,128]{2,1,0:T(8,128)(2,1)} %pad_maximum_fusion.4.rest_4_), channel_id=1, source_target_pairs={{0,8},{4,12},{24,16},{28,20},{1,9},{5,13},{25,17},{29,21},{2,10},{... | collective-permute-start | bytes 1572872 | tf_op jit(solution)/shard_map/ppermute | solution.py:561
  63.3 124.9 %copy-start.6 = (bf16[1024,512]{1,0:T(8,128)(2,1)}, bf16[1024,512]{1,0:T(8,128)(2,1)S(1)}, u32[]{:S(2)}) copy-start(bf16[1024,512]{1,0:T(8,128)(2,1)S(1)} %slice.75.rest_0_) | copy-start | bytes 3145732
  87.9 22.0 %collective-permute-start.6 = (bf16[2,128,1024]{2,1,0:T(8,128)(2,1)}, bf16[2,128,1024]{2,1,0:T(8,128)(2,1)}, u32[]{:S(2)}, u32[]{:S(2)}) collective-permute-start(bf16[2,128,1024]{2,1,0:T(8,128)(2,1)} %broadcast_select_fusion), channel_id=1, source_target_pairs={{0,8},{4,12},{1,9},{5,13},{2,10},{6,14},{3,11},{7,15}} | collective-permute-start | bytes 1572872 | tf_op jit(solution)/shard_map/ppermute | solution.py:561
  93.0 8.6 %collective-permute-start.29 = (bf16[2,1024,128]{2,1,0:T(8,128)(2,1)}, bf16[2,1024,128]{2,1,0:T(8,128)(2,1)}, u32[]{:S(2)}, u32[]{:S(2)}) collective-permute-start(bf16[2,1024,128]{2,1,0:T(8,128)(2,1)} %collective-permute-done.27.rest_5_), channel_id=1, source_target_pairs={{8,16},{12,20},{16,8},{20,12},{9,17},{13,21},{17,9},{21,13},{10,18... | collective-permute-start | bytes 1572872 | tf_op jit(solution)/shard_map/ppermute | solution.py:561
  94.5 95.5 %collective-permute-start.17 = (bf16[1024,512]{1,0:T(8,128)(2,1)S(1)}, bf16[1024,512]{1,0:T(8,128)(2,1)}, u32[]{:S(2)}, u32[]{:S(2)}) collective-permute-start(bf16[1024,512]{1,0:T(8,128)(2,1)S(1)} %slice.75.rest_0_), channel_id=1, source_target_pairs={{0,12},{4,8},{24,20},{28,16},{1,13},{5,9},{25,21},{29,17},{2,14},{... | collective-permute-start | bytes 3145736 | tf_op jit(solution)/shard_map/ppermute | solution.py:561
  97.7 93.1 %collective-permute-start.16 = (bf16[1024,512]{1,0:T(8,128)(2,1)S(1)}, bf16[1024,512]{1,0:T(8,128)(2,1)}, u32[]{:S(2)}, u32[]{:S(2)}) collective-permute-start(bf16[1024,512]{1,0:T(8,128)(2,1)S(1)} %slice.75.rest_0_), channel_id=1, source_target_pairs={{8,12},{12,8},{16,20},{20,16},{9,13},{13,9},{17,21},{21,17},{10,14... | collective-permute-start | bytes 3145736 | tf_op jit(solution)/shard_map/ppermute | solution.py:561
  101.7 90.2 %collective-permute-start.15 = (bf16[1024,512]{1,0:T(8,128)(2,1)S(1)}, bf16[1024,512]{1,0:T(8,128)(2,1)}, u32[]{:S(2)}, u32[]{:S(2)}) collective-permute-start(bf16[1024,512]{1,0:T(8,128)(2,1)S(1)} %slice.75.rest_0_), channel_id=1, source_target_pairs={{0,8},{4,12},{24,16},{28,20},{1,9},{5,13},{25,17},{29,21},{2,10},{... | collective-permute-start | bytes 3145736 | tf_op jit(solution)/shard_map/ppermute | solution.py:561
  109.8 424.1 %collective-permute-start.42 = (bf16[1024,4096]{1,0:T(8,128)(2,1)}, bf16[1024,4096]{1,0:T(8,128)(2,1)}, u32[]{:S(2)}, u32[]{:S(2)}) collective-permute-start(bf16[1024,4096]{1,0:T(8,128)(2,1)} %refs_12_.1), channel_id=1, source_target_pairs={{0,1},{1,0},{2,3},{3,2},{4,5},{5,4},{6,7},{7,6},{8,9},{9,8},{10,11... | collective-permute-start | bytes 25165832 | tf_op jit(solution)/shard_map/ppermute | solution.py:564
  183.8 350.2 %collective-permute-start.44 = (bf16[1024,4096]{1,0:T(8,128)(2,1)}, bf16[1024,4096]{1,0:T(8,128)(2,1)}, u32[]{:S(2)}, u32[]{:S(2)}) collective-permute-start(bf16[1024,4096]{1,0:T(8,128)(2,1)} %collective-permute-done.43.refs_14_), channel_id=1, source_target_pairs={{0,1},{1,0},{2,3},{3,2},{4,5},{5,4},{6,7},{7,6},{8,9},{9,8},{10,11... | collective-permute-start | bytes 25165832 | tf_op jit(solution)/shard_map/ppermute | solution.py:564
  190.0 3.5 collective-permute-start.7
  190.7 4.3 collective-permute-start.30
  191.9 29.0 %collective-permute-start.31 = (bf16[1024,256]{1,0:T(8,128)(2,1)S(1)}, bf16[1024,256]{1,0:T(8,128)(2,1)S(1)}, u32[]{:S(2)}, u32[]{:S(2)}) collective-permute-start(bf16[1024,256]{1,0:T(8,128)(2,1)S(1)} %copy-done.30), channel_id=1, source_target_pairs={{8,0},{12,4},{16,24},{20,28},{9,1},{13,5},{17,25},{21,29},{10,2},{... | collective-permute-start | bytes 1572872 | tf_op jit(solution)/shard_map/ppermute | solution.py:561
  193.6 36.1 %collective-permute-start.32 = (bf16[1024,256]{1,0:T(8,128)(2,1)S(1)}, bf16[1024,256]{1,0:T(8,128)(2,1)S(1)}, u32[]{:S(2)}, u32[]{:S(2)}) collective-permute-start(bf16[1024,256]{1,0:T(8,128)(2,1)S(1)} %copy-done.29), channel_id=1, source_target_pairs={{12,0},{8,4},{20,24},{16,28},{13,1},{9,5},{21,25},{17,29},{14,2},{... | collective-permute-start | bytes 1572872 | tf_op jit(solution)/shard_map/ppermute | solution.py:561
  195.1 103.1 %collective-permute-start.18 = (bf16[2,1024,512]{2,1,0:T(8,128)(2,1)S(1)}, bf16[2,1024,512]{2,1,0:T(8,128)(2,1)}, u32[]{:S(2)}, u32[]{:S(2)}) collective-permute-start(bf16[2,1024,512]{2,1,0:T(8,128)(2,1)S(1)} %pad_maximum_fusion.rest_4_), channel_id=1, source_target_pairs={{0,8},{4,12},{24,16},{28,20},{1,9},{5,13},{25,17},{29,21},{2,10},{... | collective-permute-start | bytes 6291464 | tf_op jit(solution)/shard_map/ppermute | solution.py:561
  220.9 95.9 %copy-start.11 = (bf16[1024,256]{1,0:T(8,128)(2,1)}, bf16[1024,256]{1,0:T(8,128)(2,1)S(1)}, u32[]{:S(2)}) copy-start(bf16[1024,256]{1,0:T(8,128)(2,1)S(1)} %collective-permute-done.31.rest_4_.rest_5_) | copy-start | bytes 1572868
  220.9 12.1 %collective-permute-start.10 = (bf16[2,1024,384]{2,1,0:T(8,128)(2,1)S(1)}, bf16[2,1024,384]{2,1,0:T(8,128)(2,1)S(1)}, u32[]{:S(2)}, u32[]{:S(2)}) collective-permute-start(bf16[2,1024,384]{2,1,0:T(8,128)(2,1)S(1)} %pad_maximum_fusion.1.rest_4_), channel_id=1, source_target_pairs={{8,16},{12,20},{16,8},{20,12},{9,17},{13,21},{17,9},{21,13},{10,18... | collective-permute-start | bytes 4718600 | tf_op jit(solution)/shard_map/ppermute | solution.py:561
  229.7 87.2 %copy-start.12 = (bf16[1024,256]{1,0:T(8,128)(2,1)}, bf16[1024,256]{1,0:T(8,128)(2,1)S(1)}, u32[]{:S(2)}) copy-start(bf16[1024,256]{1,0:T(8,128)(2,1)S(1)} %collective-permute-done.32.rest_6_.rest_7_) | copy-start | bytes 1572868
  229.7 67.8 %collective-permute-start.9 = (bf16[2,1024,384]{2,1,0:T(8,128)(2,1)S(1)}, bf16[2,1024,384]{2,1,0:T(8,128)(2,1)}, u32[]{:S(2)}, u32[]{:S(2)}) collective-permute-start(bf16[2,1024,384]{2,1,0:T(8,128)(2,1)S(1)} %pad_maximum_fusion.1.rest_4_), channel_id=1, source_target_pairs={{0,8},{4,12},{24,16},{28,20},{1,9},{5,13},{25,17},{29,21},{2,10},{... | collective-permute-start | bytes 4718600 | tf_op jit(solution)/shard_map/ppermute | solution.py:561
  233.0 87.9 %collective-permute-start.19 = (bf16[2,1024,512]{2,1,0:T(8,128)(2,1)S(1)}, bf16[2,1024,512]{2,1,0:T(8,128)(2,1)}, u32[]{:S(2)}, u32[]{:S(2)}) collective-permute-start(bf16[2,1024,512]{2,1,0:T(8,128)(2,1)S(1)} %pad_maximum_fusion.rest_4_), channel_id=1, source_target_pairs={{8,16},{12,20},{16,8},{20,12},{9,17},{13,21},{17,9},{21,13},{10,18... | collective-permute-start | bytes 6291464 | tf_op jit(solution)/shard_map/ppermute | solution.py:561
  297.5 2.7 collective-permute-start.8
  298.2 33.0 %collective-permute-start.20 = (bf16[2,1024,512]{2,1,0:T(8,128)(2,1)}, bf16[2,1024,512]{2,1,0:T(8,128)(2,1)}, u32[]{:S(2)}, u32[]{:S(2)}) collective-permute-start(bf16[2,1024,512]{2,1,0:T(8,128)(2,1)} %collective-permute-done.18.rest_5_), channel_id=1, source_target_pairs={{8,16},{12,20},{16,8},{20,12},{9,17},{13,21},{17,9},{21,13},{10,18... | collective-permute-start | bytes 6291464 | tf_op jit(solution)/shard_map/ppermute | solution.py:561
  300.2 23.8 %collective-permute-start.11 = (bf16[2,1024,384]{2,1,0:T(8,128)(2,1)}, bf16[2,1024,384]{2,1,0:T(8,128)(2,1)}, u32[]{:S(2)}, u32[]{:S(2)}) collective-permute-start(bf16[2,1024,384]{2,1,0:T(8,128)(2,1)} %collective-permute-done.9.rest_5_), channel_id=1, source_target_pairs={{8,16},{12,20},{16,8},{20,12},{9,17},{13,21},{17,9},{21,13},{10,18... | collective-permute-start | bytes 4718600 | tf_op jit(solution)/shard_map/ppermute | solution.py:561
  320.9 1.5 collective-permute-start.35
  322.4 6.7 %collective-permute-start.38 = (bf16[256,128]{1,0:T(8,128)(2,1)}, bf16[256,128]{1,0:T(8,128)(2,1)S(1)}, u32[]{:S(2)}, u32[]{:S(2)}) collective-permute-start(bf16[256,128]{1,0:T(8,128)(2,1)} %get-tuple-element.53), channel_id=1, source_target_pairs={{0,2},{1,3},{2,0},{3,1},{4,6},{5,7},{6,4},{7,5},{8,10},{9,11},{10,... | collective-permute-start | bytes 196616 | tf_op jit(solution)/shard_map/ppermute | solution.py:564
  324.0 6.0 %collective-permute-start.41 = (bf16[256,128]{1,0:T(8,128)(2,1)}, bf16[256,128]{1,0:T(8,128)(2,1)S(1)}, u32[]{:S(2)}, u32[]{:S(2)}) collective-permute-start(bf16[256,128]{1,0:T(8,128)(2,1)} %get-tuple-element.56), channel_id=1, source_target_pairs={{0,3},{1,2},{2,1},{3,0},{4,7},{5,6},{6,5},{7,4},{8,11},{9,10},{10,... | collective-permute-start | bytes 196616 | tf_op jit(solution)/shard_map/ppermute | solution.py:564
  329.2 9.5 %collective-permute-start.12 = (bf16[1024,512]{1,0:T(8,128)(2,1)}, bf16[1024,512]{1,0:T(8,128)(2,1)S(1)}, u32[]{:S(2)}, u32[]{:S(2)}) collective-permute-start(bf16[1024,512]{1,0:T(8,128)(2,1)} %get-tuple-element.34), channel_id=1, source_target_pairs={{8,12},{12,8},{16,20},{20,16},{9,13},{13,9},{17,21},{21,17},{10,14... | collective-permute-start | bytes 3145736 | tf_op jit(solution)/shard_map/ppermute | solution.py:561
  329.9 102.1 %collective-permute-start.13 = (bf16[1024,512]{1,0:T(8,128)(2,1)}, bf16[1024,512]{1,0:T(8,128)(2,1)S(1)}, u32[]{:S(2)}, u32[]{:S(2)}) collective-permute-start(bf16[1024,512]{1,0:T(8,128)(2,1)} %get-tuple-element.35), channel_id=1, source_target_pairs={{8,0},{12,4},{16,24},{20,28},{9,1},{13,5},{17,25},{21,29},{10,2},{... | collective-permute-start | bytes 3145736 | tf_op jit(solution)/shard_map/ppermute | solution.py:561
  331.3 123.3 %collective-permute-start.14 = (bf16[1024,512]{1,0:T(8,128)(2,1)}, bf16[1024,512]{1,0:T(8,128)(2,1)}, u32[]{:S(2)}, u32[]{:S(2)}) collective-permute-start(bf16[1024,512]{1,0:T(8,128)(2,1)} %get-tuple-element.36), channel_id=1, source_target_pairs={{12,0},{8,4},{20,24},{16,28},{13,1},{9,5},{21,25},{17,29},{14,2},{... | collective-permute-start | bytes 3145736 | tf_op jit(solution)/shard_map/ppermute | solution.py:561
  339.6 123.0 %collective-permute-start.21 = (bf16[1024,640]{1,0:T(8,128)(2,1)}, bf16[1024,640]{1,0:T(8,128)(2,1)S(1)}, u32[]{:S(2)}, u32[]{:S(2)}) collective-permute-start(bf16[1024,640]{1,0:T(8,128)(2,1)} %get-tuple-element.39), channel_id=1, source_target_pairs={{8,12},{12,8},{16,20},{20,16},{9,13},{13,9},{17,21},{21,17},{10,14... | collective-permute-start | bytes 3932168 | tf_op jit(solution)/shard_map/ppermute | solution.py:561
  433.0 49.5 %collective-permute-start.22 = (bf16[1024,640]{1,0:T(8,128)(2,1)}, bf16[1024,640]{1,0:T(8,128)(2,1)S(1)}, u32[]{:S(2)}, u32[]{:S(2)}) collective-permute-start(bf16[1024,640]{1,0:T(8,128)(2,1)} %get-tuple-element.40), channel_id=1, source_target_pairs={{8,0},{12,4},{16,24},{20,28},{9,1},{13,5},{17,25},{21,29},{10,2},{... | collective-permute-start | bytes 3932168 | tf_op jit(solution)/shard_map/ppermute | solution.py:561
  454.5 56.2 %collective-permute-start.23 = (bf16[1024,640]{1,0:T(8,128)(2,1)}, bf16[1024,640]{1,0:T(8,128)(2,1)}, u32[]{:S(2)}, u32[]{:S(2)}) collective-permute-start(bf16[1024,640]{1,0:T(8,128)(2,1)} %get-tuple-element.41), channel_id=1, source_target_pairs={{12,0},{8,4},{20,24},{16,28},{13,1},{9,5},{21,25},{17,29},{14,2},{... | collective-permute-start | bytes 3932168 | tf_op jit(solution)/shard_map/ppermute | solution.py:561
  462.6 57.2 %collective-permute-start.33 = (bf16[256,384]{1,0:T(8,128)(2,1)}, bf16[256,384]{1,0:T(8,128)(2,1)S(1)}, u32[]{:S(2)}, u32[]{:S(2)}) collective-permute-start(bf16[256,384]{1,0:T(8,128)(2,1)} %get-tuple-element.48), channel_id=1, source_target_pairs={{0,1},{1,0},{2,3},{3,2},{4,5},{5,4},{6,7},{7,6},{8,9},{9,8},{10,11... | collective-permute-start | bytes 589832 | tf_op jit(solution)/shard_map/ppermute | solution.py:564
  482.6 38.1 %collective-permute-start.36 = (bf16[256,384]{1,0:T(8,128)(2,1)}, bf16[256,384]{1,0:T(8,128)(2,1)S(1)}, u32[]{:S(2)}, u32[]{:S(2)}) collective-permute-start(bf16[256,384]{1,0:T(8,128)(2,1)} %get-tuple-element.51), channel_id=1, source_target_pairs={{0,2},{1,3},{2,0},{3,1},{4,6},{5,7},{6,4},{7,5},{8,10},{9,11},{10,... | collective-permute-start | bytes 589832 | tf_op jit(solution)/shard_map/ppermute | solution.py:564
  510.7 10.2 %collective-permute-start.39 = (bf16[256,384]{1,0:T(8,128)(2,1)}, bf16[256,384]{1,0:T(8,128)(2,1)S(1)}, u32[]{:S(2)}, u32[]{:S(2)}) collective-permute-start(bf16[256,384]{1,0:T(8,128)(2,1)} %get-tuple-element.54), channel_id=1, source_target_pairs={{0,3},{1,2},{2,1},{3,0},{4,7},{5,6},{6,5},{7,4},{8,11},{9,10},{10,... | collective-permute-start | bytes 589832 | tf_op jit(solution)/shard_map/ppermute | solution.py:564
  519.8 2.3 collective-permute-start.34
  520.7 9.4 %collective-permute-start.37 = (bf16[256,512]{1,0:T(8,128)(2,1)}, bf16[256,512]{1,0:T(8,128)(2,1)S(1)}, u32[]{:S(2)}, u32[]{:S(2)}) collective-permute-start(bf16[256,512]{1,0:T(8,128)(2,1)} %get-tuple-element.52), channel_id=1, source_target_pairs={{0,2},{1,3},{2,0},{3,1},{4,6},{5,7},{6,4},{7,5},{8,10},{9,11},{10,... | collective-permute-start | bytes 786440 | tf_op jit(solution)/shard_map/ppermute | solution.py:564
  520.9 13.0 %collective-permute-start.40 = (bf16[256,512]{1,0:T(8,128)(2,1)}, bf16[256,512]{1,0:T(8,128)(2,1)S(1)}, u32[]{:S(2)}, u32[]{:S(2)}) collective-permute-start(bf16[256,512]{1,0:T(8,128)(2,1)} %get-tuple-element.55), channel_id=1, source_target_pairs={{0,3},{1,2},{2,1},{3,0},{4,7},{5,6},{6,5},{7,4},{8,11},{9,10},{10,... | collective-permute-start | bytes 786440 | tf_op jit(solution)/shard_map/ppermute | solution.py:564
  (32 other events, 659.1 us)

commit v2 on v1

--- a/solution.py
+++ b/solution.py
@@ -202,9 +202,9 @@
 
 LOG2E = 1.4426950408889634
 LAYERS = 4
-CHUNKS = (3, 4, 1)
+CHUNKS = (3, 3, 2)
 LANES = 128
-PIECE = 16
+SPARE = 32
 GROUP = 4
 NEAR_GROUP = 8
 
@@ -235,33 +235,55 @@
     return pl.ds(pl.multiple_of(start, BLOCK), size)
 
 
-def keep(stats, rows, count, step, top, total):
-    lane = lax.broadcasted_iota(jnp.int32, (count, LANES), 1)
-    both = jnp.where(lane < 3 * PIECE, top, total)
-    stats[rows, :] = jnp.where(lane % PIECE == step, both, stats[rows, :])
-
-
-def pieces(value, heads):
-    lane = lax.broadcasted_iota(jnp.int32, value.shape, 1)
+def lane_of(shape):
+    return lax.broadcasted_iota(jnp.int32, shape, 1)
+
+
+def lanes_for(lane, span, head):
+    mine = lane == head
+    for part in range(1, 6):
+        mine = jnp.logical_or(mine, lane == part * span + head)
+    return mine
+
+
+def keep(stats, rows, mine, is_top, top, total):
+    stats[rows, :] = jnp.where(mine, jnp.where(is_top, top, total), stats[rows, :])
+
+
+def pieces(value, span):
+    lane = lane_of(value.shape)
     high = value.astype(jnp.bfloat16).astype(jnp.float32)
     middle = (value - high).astype(jnp.bfloat16).astype(jnp.float32)
-    turn = lane // PIECE % 3
-    part = jnp.where(turn == 0, high, jnp.where(turn == 1, middle, value - high - middle))
-    used = jnp.logical_and(lane % PIECE < heads, lane < 6 * PIECE)
-    return jnp.where(used, part, 0.0).astype(jnp.bfloat16)
-
-
-def unpieced(value, head):
-    row = lax.broadcasted_iota(jnp.int32, (LANES, LANES), 0)
-    mine = row % PIECE == head
+    low = value - high - middle
+    out = jnp.zeros_like(value)
+    for part in range(6):
+        here = jnp.logical_and(lane >= part * span, lane < (part + 1) * span)
+        out = jnp.where(here, (high, middle, low)[part % 3], out)
+    return out
+
+
+def unpieced(value, span, head):
+    row = lax.broadcasted_iota(jnp.int32, (value.shape[1], LANES), 0)
+    mine = lanes_for(row, span, head)
+    is_top = row < 3 * span
     return [
         jnp.dot(
             value,
-            jnp.where(jnp.logical_and(mine, row // (3 * PIECE) == side), 1.0, 0.0).astype(jnp.bfloat16),
+            jnp.where(jnp.logical_and(mine, side), 1.0, 0.0).astype(jnp.bfloat16),
             preferred_element_type=jnp.float32,
         )
-        for side in range(2)
+        for side in (is_top, jnp.logical_not(is_top))
     ]
+
+
+def spare_places(token_count, heads):
+    return [
+        (token_count + n // heads * SPARE, n % heads * LANES, n * LANES) for n in range(token_count // LANES)
+    ]
+
+
+def spare_rows(token_count, heads):
+    return -(-(token_count // LANES) // heads) * SPARE
 
 
 def near_attention(params, queries, key_rows, value_rows, before, after, tokens, total_blocks):
@@ -278,6 +300,8 @@
             wide[side, BLOCK + token_count : 2 * BLOCK + token_count, :] = after_ref[side]
         place = lax.broadcasted_iota(jnp.int32, (1, window + GLOBAL), 1) // BLOCK
         seq_index = par[0]
+        lane = lane_of((BLOCK, LANES))
+        mine, is_top = lanes_for(lane, heads, step), lane < 3 * heads
 
         def some_blocks(turn, _):
             numbers = [turn * NEAR_GROUP + i for i in range(NEAR_GROUP)]
@@ -303,14 +327,14 @@
             for rows, block, (top, total, context) in zip(here, blocks, found):
                 out_ref[rows, :] = context
                 top = jnp.where(block < GLOBAL // BLOCK, masked_score, top)
-                keep(stats, rows, BLOCK, step, top, total)
+                keep(stats, rows, mine, is_top, top, total)
             return 0
 
         lax.fori_loop(0, blocks_here // NEAR_GROUP, some_blocks, 0)
 
         @pl.when(step == heads - 1)
         def _():
-            piece_ref[...] = pieces(stats[...], heads)
+            piece_ref[...] = pieces(stats[...], heads).astype(jnp.bfloat16)
 
     column = pl.BlockSpec((token_count, HEAD_DIM), lambda h, par: (0, h))
     edge = pl.BlockSpec((2, BLOCK, HEAD_DIM), lambda h, par: (0, 0, h))
@@ -346,6 +370,7 @@
     column_tokens = len(pairs) * token_count
     asked = RANDOM * BLOCK
     callers = len(queries)
+    rows_sent = token_count + spare_rows(token_count, heads)
 
     def body(par, *rest):
         query_refs = rest[:callers]
@@ -383,9 +408,14 @@
             columns = pl.ds(pl.multiple_of(step * HEAD_DIM, HEAD_DIM), HEAD_DIM)
             place = lax.broadcasted_iota(jnp.int32, (1, asked), 1) // BLOCK
 
+            masks = {}
+            for count in (BLOCK, GLOBAL):
+                lane = lane_of((count, LANES))
+                masks[count] = lanes_for(lane, heads, step), lane < 3 * heads
+
             def store(caller, rows, count, top, total, context):
                 outs[caller][rows, columns] = context.astype(jnp.bfloat16)
-                keep(stats.at[caller], rows, count, step, top, total)
+                keep(stats.at[caller], rows, *masks[count], top, total)
 
             def some_blocks(turn, _):
                 chosen = [(caller, turn * GROUP + i) for i in range(GROUP) for caller in range(callers)]
@@ -409,8 +439,7 @@
 
             lax.fori_loop(0, blocks_here // GROUP, some_blocks, 0)
 
-            for caller in range(callers):
-
+            def ends_of_line(caller):
                 @pl.when(par[names["device"] + caller] == 0)
                 def _():
                     query = query_refs[caller][0:GLOBAL, :]
@@ -425,9 +454,15 @@
                     context = sum(part[2] * share for part, share in zip(found, shares))
                     store(caller, slice(0, GLOBAL), GLOBAL, joint, total, context)
 
+            for caller in range(callers):
+                if caller % 2:
+                    ends_of_line(caller)
+
                 @pl.when(step == heads - 1)
                 def _():
-                    outs[caller][:, width:] = pieces(stats[caller], heads)
+                    for row, column, token in spare_places(token_count, heads):
+                        part = jnp.transpose(pieces(stats[caller, token : token + LANES, :], heads))
+                        outs[caller][row : row + SPARE, column : column + LANES] = part[:SPARE].astype(jnp.bfloat16)
 
         pl.when(par[names["inner"]] == 1)(work)
 
@@ -438,14 +473,14 @@
             grid=(heads,),
             in_specs=[pl.BlockSpec((token_count, HEAD_DIM), lambda h, par: (0, h))] * callers
             + [pl.BlockSpec(memory_space=pl.ANY)] * len(pairs),
-            out_specs=[pl.BlockSpec((token_count, width + LANES), lambda h, par: (0, 0))] * callers,
+            out_specs=[pl.BlockSpec((rows_sent, width), lambda h, par: (0, 0))] * callers,
             scratch_shapes=[
                 pltpu.VMEM((2, 2, column_tokens, HEAD_DIM), jnp.bfloat16),
                 pltpu.VMEM((callers, token_count, LANES), jnp.float32),
                 pltpu.SemaphoreType.DMA((2, len(pairs))),
             ],
         ),
-        out_shape=[jax.ShapeDtypeStruct((token_count, width + LANES), jnp.bfloat16)] * callers,
+        out_shape=[jax.ShapeDtypeStruct((rows_sent, width), jnp.bfloat16)] * callers,
         compiler_params=pltpu.CompilerParams(dimension_semantics=("arbitrary",)),
         cost_estimate=pl.CostEstimate(
             flops=4 * width * token_count * callers * asked, bytes_accessed=4 * column_tokens * width, transcendentals=0
@@ -455,22 +490,31 @@
 
 def merge(params, near, near_lse, inner_pair, outer_pair, first_head, names, head_count):
     token_count = near.shape[0]
-    width = inner_pair[0].shape[1] - LANES
+    rows_sent, width = inner_pair[0].shape
     heads = width // HEAD_DIM
     quarter = token_count // head_count
     some = inner_pair + outer_pair
 
     def body(par, near_ref, lse_ref, *rest):
-        parts = rest[: 2 * len(some)]
-        outs = rest[2 * len(some) : -1]
-        done = rest[-1]
+        parts = rest[: len(some)]
+        outs = rest[len(some) : -2]
+        stats, done = rest[-2:]
         step = pl.program_id(0)
 
         def join(group):
-            found = [unpieced(lse_ref[...], first_head + step) + [near_ref[...]]]
-            for number in group:
-                context = parts[2 * number][...].astype(jnp.float32)
-                found.append(unpieced(parts[2 * number + 1][...], step) + [context])
+            @pl.when(step == 0)
+            def _():
+                for side, number in enumerate(group):
+                    for row, column, token in spare_places(token_count, heads):
+                        part = parts[number][row : row + SPARE, column : column + LANES].astype(jnp.float32)
+                        stats[side, token : token + LANES, :] = jnp.transpose(part)
+
+            columns = pl.ds(pl.multiple_of(step * HEAD_DIM, HEAD_DIM), HEAD_DIM)
+            all_heads = near.shape[1] // HEAD_DIM
+            found = [unpieced(lse_ref[...], all_heads, first_head + step) + [near_ref[...]]]
+            for side, number in enumerate(group):
+                context = parts[number][0:token_count, columns].astype(jnp.float32)
+                found.append(unpieced(stats[side].astype(jnp.bfloat16), heads, step) + [context])
             top = jnp.maximum(jnp.maximum(found[0][0], found[1][0]), found[2][0])
             shares = [jnp.exp2((part[0] - top) * FACTOR) for part in found]
             total = sum(part[1] * share for part, share in zip(found, shares))
@@ -483,10 +527,6 @@
             start = jnp.bitwise_xor(par[names["head"]], number) * quarter
             outs[number][...] = done[pl.ds(pl.multiple_of(start, quarter), quarter), :]
 
-    part_specs = [
-        pl.BlockSpec((token_count, HEAD_DIM), lambda h, par: (0, h)),
-        pl.BlockSpec((token_count, LANES), lambda h, par: (0, heads)),
-    ]
     return pl.pallas_call(
         body,
         grid_spec=pltpu.PrefetchScalarGridSpec(
@@ -496,43 +536,47 @@
                 pl.BlockSpec((token_count, HEAD_DIM), lambda h, par: (0, first_head + h)),
                 pl.BlockSpec((token_count, LANES), lambda h, par: (0, 0)),
             ]
-            + part_specs * len(some),
+            + [pl.BlockSpec((rows_sent, width), lambda h, par: (0, 0))] * len(some),
             out_specs=[pl.BlockSpec((quarter, HEAD_DIM), lambda h, par: (0, h))] * head_count,
-            scratch_shapes=[pltpu.VMEM((token_count, HEAD_DIM), jnp.bfloat16)],
+            scratch_shapes=[
+                pltpu.VMEM((2, token_count, SPARE), jnp.float32),
+                pltpu.VMEM((token_count, HEAD_DIM), jnp.bfloat16),
+            ],
         ),
         out_shape=[jax.ShapeDtypeStruct((quarter, width), jnp.bfloat16)] * head_count,
         compiler_params=pltpu.CompilerParams(dimension_semantics=("arbitrary",)),
         cost_estimate=pl.CostEstimate(flops=64 * token_count * width, bytes_accessed=8 * token_count * width, transcendentals=0),
-    )(params, near, near_lse, *[part for part in some for _ in range(2)])
-
-
-def project(parts, weights, row_starts, tile=512):
+    )(params, near, near_lse, *some)
+
+
+def project(parts, weights, tile=512):
     rows = parts[0][0].shape[0]
-    depth, width = weights[0].shape
-    chunks = len(row_starts)
+    width = weights[0].shape[1]
+    chunks = len(parts[0])
+    depth = sum(part.shape[1] for part in parts[0])
+    sides = len(weights)
 
     def body(*refs):
-        part_refs = refs[: len(weights) * chunks]
-        weight_refs = refs[len(weights) * chunks : -1]
+        part_refs = refs[: sides * chunks]
+        weight_refs = refs[sides * chunks : sides * chunks + sides]
         total = jnp.zeros((rows, tile), jnp.float32)
         for number, weight in enumerate(weight_refs):
-            left = jnp.concatenate(
-                [part_refs[number * chunks + c][...] for c in range(chunks)], axis=1
-            )
+            left = [part_refs[number * chunks + c][...] for c in range(chunks)]
+            left = jnp.concatenate(left, axis=1)
             total = total + jnp.dot(left, weight[...], preferred_element_type=jnp.float32)
-        refs[-1][...] = total.astype(jnp.bfloat16)
+        refs[-1][...] = total.astype(refs[-1].dtype)
 
     flat = [part for group in parts for part in group]
     return pl.pallas_call(
         body,
         grid=(width // tile,),
         in_specs=[pl.BlockSpec(part.shape, lambda n: (0, 0)) for part in flat]
-        + [pl.BlockSpec((depth, tile), lambda n: (0, n))] * len(weights),
+        + [pl.BlockSpec((depth, tile), lambda n: (0, n))] * sides,
         out_specs=pl.BlockSpec((rows, tile), lambda n: (0, n)),
         out_shape=jax.ShapeDtypeStruct((rows, width), jnp.bfloat16),
         compiler_params=pltpu.CompilerParams(dimension_semantics=("arbitrary",)),
         cost_estimate=pl.CostEstimate(
-            flops=2 * rows * depth * len(weights) * width, bytes_accessed=2 * depth * len(weights) * width, transcendentals=0
+            flops=2 * rows * depth * sides * width, bytes_accessed=2 * depth * sides * width, transcendentals=0
         ),
         name="project",
     )(*flat, *weights)
@@ -551,9 +595,8 @@
     mirror = last - layer
     ends = ((0, 1), (last, last - 1))
     to_inner = [(2 * a + x, 2 * b + x) for a, b in ends for x in range(2)]
-    to_inner_across = [(2 * a + x, 2 * b + 1 - x) for a, b in ends for x in range(2)]
     to_outer = [(b, a) for a, b in to_inner]
-    to_outer_across = [(b, a) for a, b in to_inner_across]
+    to_outer_across = [(2 * b + x, 2 * a + 1 - x) for a, b in ends for x in range(2)]
     middle = [(2 * a + x, 2 * (last - a) + x) for _, a in ends for x in range(2)]
     across = [(2 * a + x, 2 * a + 1 - x) for _, a in ends for x in range(2)]
 
@@ -593,7 +636,9 @@
             query = jnp.concatenate([query, jnp.pad(listed, ((0, 0), spare))], axis=0)
         outer_pair = move(pair, to_inner)
         mirror_pair = move(pair, middle)
-        callers = [query, move(query, to_inner), move(query, across), move(query, to_inner_across)]
+        from_outer = move(query, to_inner)
+        from_side = move(query, across)
+        callers = [query, from_outer, from_side, move(from_outer, across)]
         mirror_outer = move(outer_pair, middle)
         moved.append((first_head, callers, [pair, outer_pair, mirror_pair, mirror_outer]))
         first_head += size
@@ -627,7 +672,7 @@
         for distance, part in enumerate(outs):
             parts[distance].append(swap(part, distance) if distance else part)
     weights = [output_weight, swap(output_weight, 1), far_weight, swap(far_weight, 1)]
-    return project(parts, weights, moved)
+    return project(parts, weights)
 
 
 def local(*arrays):

time: 554 us -> 552 us (level)
    ppermute x33, waiting for transfers between devices: 252 us -> 194 us  [move(): return lax.ppermute(array, 'seq', pairs)]
    ppermute x12, waiting for transfers between devices: 87.2 us -> 140 us  [swap(): lax.ppermute(array, 'head', [(i, i ^ distance) for i in range(head_count)])]
  transfers between devices with their start and end apart: 45 -> 45, of which waited for: 12 -> 19; matrix products, arithmetic and copies ran while one was open for 4% -> 4% of each run, Pallas kernels for 8% -> 8%
where the time goes in v2:
time: 552 us; the launch traced here: 550 us
  waiting for transfers between devices  334 us (61%)
  starting transfers between devices  127 us (23%)
  Pallas kernels  63.1 us (11%)
  other arithmetic  12.9 us (2%)
  local copies, waits for them, and re-layouts  12 us (2%)
    ppermute x33, waiting for transfers between devices, move(): return lax.ppermute(array, 'seq', pairs)  194 us
    ppermute x12, waiting for transfers between devices, swap(): lax.ppermute(array, 'head', [(i, i ^ distance) for i in range(head_count)])  140 us
    ppermute x33, starting transfers between devices, move(): return lax.ppermute(array, 'seq', pairs)  115 us
    pallas_call x3, Pallas kernels, merge(): pl.pallas_call(body, grid_spec=pltpu.PrefetchScalarGridSpec(num_scalar_pr...  19 us
    pallas_call x1, Pallas kernels, project(): pl.pallas_call(body, grid=(width // tile,), in_specs=[pl.BlockSpec(part.s...  17.6 us
    pallas_call x3, Pallas kernels, column_attention(): pl.pallas_call(body, grid_spec=pltpu.PrefetchScalarGridSpec(num_scalar_pr...  13.8 us
    pallas_call x1, Pallas kernels, near_attention(): pl.pallas_call(body, grid_spec=pltpu.PrefetchScalarGridSpec(num_scalar_pr...  12.7 us
    ppermute x12, starting transfers between devices, swap(): lax.ppermute(array, 'head', [(i, i ^ distance) for i in range(head_count)])  11.5 us
  transfers between devices with their start and end apart: 45, of which 19 were waited for; matrix products, arithmetic and copies ran while one was open for 4% of the time, Pallas kernels for 8%

profile of v2, /device:TPU:0, one launch (start us, length us, event | category | flops | bytes accessed | tf_op | source)
XLA Modules:
  0.0 549.6 jit_solution(15063232056325655269)
XLA Ops:
  0.0 3.0 collective-permute-start.43
  4.2 3.4 collective-permute-start.3
  9.5 4.3 collective-permute-start.5
  18.5 1.7 collective-permute-start.16
  20.2 2.7 collective-permute-done.4.after_ref
  22.9 3.6 collective-permute-start.24
  26.9 2.9 collective-permute-done.5
  29.8 2.2 collective-permute-start.15
  32.0 2.1 pad_maximum_fusion.3.rest_0_
  34.1 1.6 collective-permute-start.1
  35.6 2.8 collective-permute-done.24.rest_1_
  38.4 5.3 collective-permute-start
  43.8 9.9 %collective-permute-start.6 = (bf16[2,128,1024]{2,1,0:T(8,128)(2,1)S(1)}, bf16[2,128,1024]{2,1,0:T(8,128)(2,1)S(1)}, u32[]{:S(2)}, u32[]{:S(2)}) collective-permute-start(bf16[2,128,1024]{2,1,0:T(8,128)(2,1)S(1)} %broadcast_select_fusion), channel_id=1, source_target_pairs={{0,8},{4,12},{1,9},{5,13},{2,10},{6,14},{3,11},{7,15}} | collective-permute-start | bytes 1572872 | tf_op jit(solution)/shard_map/ppermute | solution.py:604
  55.2 128.6 %collective-permute-done.43.refs_14_ = bf16[1024,4096]{1,0:T(8,128)(2,1)} collective-permute-done((bf16[1024,4096]{1,0:T(8,128)(2,1)}, bf16[1024,4096]{1,0:T(8,128)(2,1)}, u32[]{:S(2)}, u32[]{:S(2)}) %collective-permute-start.43) | collective-permute-done | bytes 8388640 | tf_op jit(solution)/shard_map/ppermute | solution.py:607
  185.3 10.2 %collective-permute-start.27 = (bf16[2,1024,256]{2,1,0:T(8,128)(2,1)S(1)}, bf16[2,1024,256]{2,1,0:T(8,128)(2,1)}, u32[]{:S(2)}, u32[]{:S(2)}) collective-permute-start(bf16[2,1024,256]{2,1,0:T(8,128)(2,1)S(1)} %pad_maximum_fusion.2.rest_4_), channel_id=1, source_target_pairs={{0,8},{4,12},{24,16},{28,20},{1,9},{5,13},{25,17},{29,21},{2,10},{... | collective-permute-start | bytes 3145736 | tf_op jit(solution)/shard_map/ppermute | solution.py:604
  195.5 1.5 slice_bitcast_fusion
  197.3 1.8 collective-permute-start.10
  201.3 15.7 %collective-permute-done.27.rest_5_ = bf16[2,1024,256]{2,1,0:T(8,128)(2,1)} collective-permute-done((bf16[2,1024,256]{2,1,0:T(8,128)(2,1)S(1)}, bf16[2,1024,256]{2,1,0:T(8,128)(2,1)}, u32[]{:S(2)}, u32[]{:S(2)}) %collective-permute-start.27) | collective-permute-done | bytes 1048608 | tf_op jit(solution)/shard_map/ppermute | solution.py:604
  217.8 1.6 collective-permute-start.2
  219.4 44.3 %collective-permute-start.9 = (bf16[2,1024,384]{2,1,0:T(8,128)(2,1)S(1)}, bf16[2,1024,384]{2,1,0:T(8,128)(2,1)}, u32[]{:S(2)}, u32[]{:S(2)}) collective-permute-start(bf16[2,1024,384]{2,1,0:T(8,128)(2,1)S(1)} %pad_maximum_fusion.rest_4_), channel_id=1, source_target_pairs={{0,8},{4,12},{24,16},{28,20},{1,9},{5,13},{25,17},{29,21},{2,10},{... | collective-permute-start | bytes 4718600 | tf_op jit(solution)/shard_map/ppermute | solution.py:604
  263.7 1.5 pad_maximum_fusion.1.rest_4_
  265.3 2.4 collective-permute-start.18
  268.4 1.7 collective-permute-start.29
  271.7 2.5 broadcast_select_fusion.2
  277.6 3.9 shard_map.104
  281.5 15.8 %collective-permute-done.9.rest_5_ = bf16[2,1024,384]{2,1,0:T(8,128)(2,1)} collective-permute-done((bf16[2,1024,384]{2,1,0:T(8,128)(2,1)S(1)}, bf16[2,1024,384]{2,1,0:T(8,128)(2,1)}, u32[]{:S(2)}, u32[]{:S(2)}) %collective-permute-start.9) | collective-permute-done | bytes 1572896 | tf_op jit(solution)/shard_map/ppermute | solution.py:604
  298.0 31.4 %collective-permute-done.18.rest_5_ = bf16[2,1024,384]{2,1,0:T(8,128)(2,1)} collective-permute-done((bf16[2,1024,384]{2,1,0:T(8,128)(2,1)S(1)}, bf16[2,1024,384]{2,1,0:T(8,128)(2,1)}, u32[]{:S(2)}, u32[]{:S(2)}) %collective-permute-start.18) | collective-permute-done | bytes 1572896 | tf_op jit(solution)/shard_map/ppermute | solution.py:604
  332.9 14.8 %collective-permute-done.31.rest_2_ = bf16[1152,256]{1,0:T(8,128)(2,1)S(1)} collective-permute-done((bf16[1152,256]{1,0:T(8,128)(2,1)}, bf16[1152,256]{1,0:T(8,128)(2,1)S(1)}, u32[]{:S(2)}, u32[]{:S(2)}) %collective-permute-start.31) | collective-permute-done | bytes 589856 | tf_op jit(solution)/shard_map/ppermute | solution.py:604
  348.6 1.8 collective-permute-start.20
  350.4 7.8 %collective-permute-done.32.rest_3_ = bf16[1152,256]{1,0:T(8,128)(2,1)} collective-permute-done((bf16[1152,256]{1,0:T(8,128)(2,1)}, bf16[1152,256]{1,0:T(8,128)(2,1)}, u32[]{:S(2)}, u32[]{:S(2)}) %collective-permute-start.32) | collective-permute-done | bytes 589856 | tf_op jit(solution)/shard_map/ppermute | solution.py:604
  358.2 1.8 collective-permute-start.11
  360.7 2.5 broadcast_select_fusion.3.token_ref
  363.2 12.7 %near.1 = (f32[1024,1024]{1,0:T(8,128)}, bf16[1024,128]{1,0:T(8,128)(2,1)}) custom-call(s32[1]{0:T(128)} %bitcast.par, bf16[1024,1024]{1,0:T(8,128)(2,1)} %query_ref.1, bf16[1024,1024]{1,0:T(8,128)(2,1)} %key_ref.1, bf16[1024,1024]{1,0:T(8,128)(2,1)} %value_ref.1, bf16[2,64,1024]{2,1,0:T(8,128)(2,1)} %copy-done.21, bf16[2,64,1024]{2,1,0:T(8,128)(2,1)} %copy-done.22, ...), custom_call_target="tpu_custom_call" | custom-call | flops 1342177280 | bytes 8388608 | tf_op jit(solution)/shard_map/near/pallas_call | solution.py:341
  375.8 5.4 shard_map.105
  381.3 1.7 collective-permute-done.35.refs_5_
  383.0 1.5 collective-permute-start.38
  384.5 5.0 shard_map.102
  393.3 5.0 shard_map.100
  399.1 57.6 %collective-permute-done.22.rest_2_ = bf16[1120,384]{1,0:T(8,128)(2,1)S(1)} collective-permute-done((bf16[1120,384]{1,0:T(8,128)(2,1)}, bf16[1120,384]{1,0:T(8,128)(2,1)S(1)}, u32[]{:S(2)}, u32[]{:S(2)}) %collective-permute-start.22) | collective-permute-done | bytes 860192 | tf_op jit(solution)/shard_map/ppermute | solution.py:604
  457.9 17.2 %collective-permute-done.23.rest_3_ = bf16[1120,384]{1,0:T(8,128)(2,1)} collective-permute-done((bf16[1120,384]{1,0:T(8,128)(2,1)}, bf16[1120,384]{1,0:T(8,128)(2,1)}, u32[]{:S(2)}, u32[]{:S(2)}) %collective-permute-start.23) | collective-permute-done | bytes 860192 | tf_op jit(solution)/shard_map/ppermute | solution.py:604
  476.7 6.8 %shard_map.103 = (bf16[256,384]{1,0:T(8,128)(2,1)}, bf16[256,384]{1,0:T(8,128)(2,1)}, bf16[256,384]{1,0:T(8,128)(2,1)}, bf16[256,384]{1,0:T(8,128)(2,1)}) custom-call(s32[267]{0:T(512)} %concatenate.29.par, f32[1024,1024]{1,0:T(8,128)} %get-tuple-element.31.near_ref, bf16[1024,128]{1,0:T(8,128)(2,1)} %get-tuple-element.32.lse_ref, ...), custom_call_target="tpu_custom_call" | custom-call | flops 25165824 | bytes 3145728 | tf_op jit(solution)/shard_map/pallas_call | solution.py:530
  484.7 8.8 %collective-permute-done.13.rest_2_ = bf16[1120,384]{1,0:T(8,128)(2,1)S(1)} collective-permute-done((bf16[1120,384]{1,0:T(8,128)(2,1)}, bf16[1120,384]{1,0:T(8,128)(2,1)S(1)}, u32[]{:S(2)}, u32[]{:S(2)}) %collective-permute-start.13) | collective-permute-done | bytes 860192 | tf_op jit(solution)/shard_map/ppermute | solution.py:604
  493.5 2.2 collective-permute-start.37
  495.7 16.3 %collective-permute-done.14.rest_3_ = bf16[1120,384]{1,0:T(8,128)(2,1)} collective-permute-done((bf16[1120,384]{1,0:T(8,128)(2,1)}, bf16[1120,384]{1,0:T(8,128)(2,1)}, u32[]{:S(2)}, u32[]{:S(2)}) %collective-permute-start.14) | collective-permute-done | bytes 860192 | tf_op jit(solution)/shard_map/ppermute | solution.py:604
  513.2 6.8 %shard_map.101 = (bf16[256,384]{1,0:T(8,128)(2,1)}, bf16[256,384]{1,0:T(8,128)(2,1)}, bf16[256,384]{1,0:T(8,128)(2,1)}, bf16[256,384]{1,0:T(8,128)(2,1)}) custom-call(s32[267]{0:T(512)} %concatenate.29.par, f32[1024,1024]{1,0:T(8,128)} %get-tuple-element.31.near_ref, bf16[1024,128]{1,0:T(8,128)(2,1)} %get-tuple-element.32.lse_ref, ...), custom_call_target="tpu_custom_call" | custom-call | flops 25165824 | bytes 3145728 | tf_op jit(solution)/shard_map/pallas_call | solution.py:530
  522.3 6.5 %collective-permute-done.36.refs_6_ = bf16[256,384]{1,0:T(8,128)(2,1)S(1)} collective-permute-done((bf16[256,384]{1,0:T(8,128)(2,1)}, bf16[256,384]{1,0:T(8,128)(2,1)S(1)}, u32[]{:S(2)}, u32[]{:S(2)}) %collective-permute-start.36) | collective-permute-done | bytes 196640 | tf_op jit(solution)/shard_map/ppermute | solution.py:607
  528.8 2.5 collective-permute-done.39.refs_9_
  532.0 17.6 %project.1 = bf16[256,4096]{1,0:T(8,128)(2,1)} custom-call(bf16[256,384]{1,0:T(8,128)(2,1)} %get-tuple-element.37.refs_0_, bf16[256,384]{1,0:T(8,128)(2,1)} %get-tuple-element.42.refs_1_, bf16[256,256]{1,0:T(8,128)(2,1)} %get-tuple-element.47.refs_2_, bf16[256,384]{1,0:T(8,128)(2,1)} %copy-done.26, bf16[256,384]{1,0:T(8,128)(2,1)} %copy-done.23, ...), custom_call_target="tpu_custom_call" | custom-call | flops 8589934592 | bytes 33554432 | tf_op jit(solution)/shard_map/project/pallas_call | solution.py:570
  (164 shorter events, 38.2 us)
Async XLA Ops:
  0.0 183.8 %collective-permute-start.43 = (bf16[1024,4096]{1,0:T(8,128)(2,1)}, bf16[1024,4096]{1,0:T(8,128)(2,1)}, u32[]{:S(2)}, u32[]{:S(2)}) collective-permute-start(bf16[1024,4096]{1,0:T(8,128)(2,1)} %refs_12_.1), channel_id=1, source_target_pairs={{0,2},{1,3},{2,0},{3,1},{4,6},{5,7},{6,4},{7,5},{8,10},{9,11},{10,... | collective-permute-start | bytes 25165832 | tf_op jit(solution)/shard_map/ppermute | solution.py:607
  4.2 14.4 %collective-permute-start.3 = (bf16[2,64,1024]{2,1,0:T(8,128)(2,1)S(1)}, bf16[2,64,1024]{2,1,0:T(8,128)(2,1)S(1)}, u32[]{:S(2)}, u32[]{:S(2)}) collective-permute-start(bf16[2,64,1024]{2,1,0:T(8,128)(2,1)S(1)} %pad_maximum_fusion.5), channel_id=1, source_target_pairs={{0,4},{4,8},{8,12},{12,16},{16,20},{20,24},{24,28},{1,5},{5,9},{9,... | collective-permute-start | bytes 786440 | tf_op jit(solution)/shard_map/ppermute | solution.py:604
  9.5 20.3 %collective-permute-start.5 = (bf16[2,128,1024]{2,1,0:T(8,128)(2,1)}, bf16[2,128,1024]{2,1,0:T(8,128)(2,1)}, u32[]{:S(2)}, u32[]{:S(2)}) collective-permute-start(bf16[2,128,1024]{2,1,0:T(8,128)(2,1)} %pad_maximum_fusion.4), channel_id=1, source_target_pairs={{0,4},{1,5},{2,6},{3,7}} | collective-permute-start | bytes 1572872 | tf_op jit(solution)/shard_map/ppermute | solution.py:604
  13.8 9.1 %collective-permute-start.4 = (bf16[2,64,1024]{2,1,0:T(8,128)(2,1)S(1)}, bf16[2,64,1024]{2,1,0:T(8,128)(2,1)S(1)}, u32[]{:S(2)}, u32[]{:S(2)}) collective-permute-start(bf16[2,64,1024]{2,1,0:T(8,128)(2,1)S(1)} %pad_maximum_fusion.6), channel_id=1, source_target_pairs={{4,0},{8,4},{12,8},{16,12},{20,16},{24,20},{28,24},{5,1},{9,5},{13... | collective-permute-start | bytes 786440 | tf_op jit(solution)/shard_map/ppermute | solution.py:604
  16.0 18.0 %collective-permute-start.25 = (bf16[1024,256]{1,0:T(8,128)(2,1)}, bf16[1024,256]{1,0:T(8,128)(2,1)}, u32[]{:S(2)}, u32[]{:S(2)}) collective-permute-start(bf16[1024,256]{1,0:T(8,128)(2,1)} %slice.78.rest_0_), channel_id=1, source_target_pairs={{8,12},{12,8},{16,20},{20,16},{9,13},{13,9},{17,21},{21,17},{10,14... | collective-permute-start | bytes 1572872 | tf_op jit(solution)/shard_map/ppermute | solution.py:604
  18.5 25.3 %collective-permute-start.16 = (bf16[1024,384]{1,0:T(8,128)(2,1)S(1)}, bf16[1024,384]{1,0:T(8,128)(2,1)}, u32[]{:S(2)}, u32[]{:S(2)}) collective-permute-start(bf16[1024,384]{1,0:T(8,128)(2,1)S(1)} %get-tuple-element.67.rest_0_), channel_id=1, source_target_pairs={{8,12},{12,8},{16,20},{20,16},{9,13},{13,9},{17,21},{21,17},{10,14... | collective-permute-start | bytes 2359304 | tf_op jit(solution)/shard_map/ppermute | solution.py:604
  22.9 15.5 %collective-permute-start.24 = (bf16[1024,256]{1,0:T(8,128)(2,1)}, bf16[1024,256]{1,0:T(8,128)(2,1)}, u32[]{:S(2)}, u32[]{:S(2)}) collective-permute-start(bf16[1024,256]{1,0:T(8,128)(2,1)} %slice.78.rest_0_), channel_id=1, source_target_pairs={{0,8},{4,12},{24,16},{28,20},{1,9},{5,13},{25,17},{29,21},{2,10},{... | collective-permute-start | bytes 1572872 | tf_op jit(solution)/shard_map/ppermute | solution.py:604
  29.8 25.4 %collective-permute-start.15 = (bf16[1024,384]{1,0:T(8,128)(2,1)S(1)}, bf16[1024,384]{1,0:T(8,128)(2,1)}, u32[]{:S(2)}, u32[]{:S(2)}) collective-permute-start(bf16[1024,384]{1,0:T(8,128)(2,1)S(1)} %get-tuple-element.67.rest_0_), channel_id=1, source_target_pairs={{0,8},{4,12},{24,16},{28,20},{1,9},{5,13},{25,17},{29,21},{2,10},{... | collective-permute-start | bytes 2359304 | tf_op jit(solution)/shard_map/ppermute | solution.py:604
  34.1 149.8 %collective-permute-start.1 = (bf16[1040,384]{1,0:T(8,128)(2,1)}, bf16[1040,384]{1,0:T(8,128)(2,1)}, u32[]{:S(2)}, u32[]{:S(2)}) collective-permute-start(bf16[1040,384]{1,0:T(8,128)(2,1)} %pad_maximum_fusion.3.rest_0_), channel_id=1, source_target_pairs={{8,12},{12,8},{16,20},{20,16},{9,13},{13,9},{17,21},{21,17},{10,14... | collective-permute-start | bytes 2396168 | tf_op jit(solution)/shard_map/ppermute | solution.py:604
  38.4 146.2 %collective-permute-start = (bf16[1040,384]{1,0:T(8,128)(2,1)}, bf16[1040,384]{1,0:T(8,128)(2,1)}, u32[]{:S(2)}, u32[]{:S(2)}) collective-permute-start(bf16[1040,384]{1,0:T(8,128)(2,1)} %pad_maximum_fusion.3.rest_0_), channel_id=1, source_target_pairs={{0,8},{4,12},{24,16},{28,20},{1,9},{5,13},{25,17},{29,21},{2,10},{... | collective-permute-start | bytes 2396168 | tf_op jit(solution)/shard_map/ppermute | solution.py:604
  43.8 151.7 %copy-start.1 = (bf16[1024,1024]{1,0:T(8,128)(2,1)S(1)}, bf16[1024,1024]{1,0:T(8,128)(2,1)}, u32[]{:S(2)}) copy-start(bf16[1024,1024]{1,0:T(8,128)(2,1)} %value_ref.1) | copy-start | bytes 6291460
  43.8 141.5 %collective-permute-start.6 = (bf16[2,128,1024]{2,1,0:T(8,128)(2,1)S(1)}, bf16[2,128,1024]{2,1,0:T(8,128)(2,1)S(1)}, u32[]{:S(2)}, u32[]{:S(2)}) collective-permute-start(bf16[2,128,1024]{2,1,0:T(8,128)(2,1)S(1)} %broadcast_select_fusion), channel_id=1, source_target_pairs={{0,8},{4,12},{1,9},{5,13},{2,10},{6,14},{3,11},{7,15}} | collective-permute-start | bytes 1572872 | tf_op jit(solution)/shard_map/ppermute | solution.py:604
  55.2 476.1 %collective-permute-start.42 = (bf16[1024,4096]{1,0:T(8,128)(2,1)}, bf16[1024,4096]{1,0:T(8,128)(2,1)}, u32[]{:S(2)}, u32[]{:S(2)}) collective-permute-start(bf16[1024,4096]{1,0:T(8,128)(2,1)} %refs_12_.1), channel_id=1, source_target_pairs={{0,1},{1,0},{2,3},{3,2},{4,5},{5,4},{6,7},{7,6},{8,9},{9,8},{10,11... | collective-permute-start | bytes 25165832 | tf_op jit(solution)/shard_map/ppermute | solution.py:607
  183.8 347.5 %collective-permute-start.44 = (bf16[1024,4096]{1,0:T(8,128)(2,1)}, bf16[1024,4096]{1,0:T(8,128)(2,1)}, u32[]{:S(2)}, u32[]{:S(2)}) collective-permute-start(bf16[1024,4096]{1,0:T(8,128)(2,1)} %collective-permute-done.43.refs_14_), channel_id=1, source_target_pairs={{0,1},{1,0},{2,3},{3,2},{4,5},{5,4},{6,7},{7,6},{8,9},{9,8},{10,11... | collective-permute-start | bytes 25165832 | tf_op jit(solution)/shard_map/ppermute | solution.py:607
  183.9 16.7 %collective-permute-start.28 = (bf16[2,1024,256]{2,1,0:T(8,128)(2,1)S(1)}, bf16[2,1024,256]{2,1,0:T(8,128)(2,1)S(1)}, u32[]{:S(2)}, u32[]{:S(2)}) collective-permute-start(bf16[2,1024,256]{2,1,0:T(8,128)(2,1)S(1)} %pad_maximum_fusion.2.rest_4_), channel_id=1, source_target_pairs={{8,16},{12,20},{16,8},{20,12},{9,17},{13,21},{17,9},{21,13},{10,18... | collective-permute-start | bytes 3145736 | tf_op jit(solution)/shard_map/ppermute | solution.py:604
  184.6 12.6 %collective-permute-start.26 = (bf16[1024,256]{1,0:T(8,128)(2,1)}, bf16[1024,256]{1,0:T(8,128)(2,1)S(1)}, u32[]{:S(2)}, u32[]{:S(2)}) collective-permute-start(bf16[1024,256]{1,0:T(8,128)(2,1)} %collective-permute-done.24.rest_1_), channel_id=1, source_target_pairs={{8,12},{12,8},{16,20},{20,16},{9,13},{13,9},{17,21},{21,17},{10,14... | collective-permute-start | bytes 1572872 | tf_op jit(solution)/shard_map/ppermute | solution.py:604
  185.3 31.7 %collective-permute-start.27 = (bf16[2,1024,256]{2,1,0:T(8,128)(2,1)S(1)}, bf16[2,1024,256]{2,1,0:T(8,128)(2,1)}, u32[]{:S(2)}, u32[]{:S(2)}) collective-permute-start(bf16[2,1024,256]{2,1,0:T(8,128)(2,1)S(1)} %pad_maximum_fusion.2.rest_4_), channel_id=1, source_target_pairs={{0,8},{4,12},{24,16},{28,20},{1,9},{5,13},{25,17},{29,21},{2,10},{... | collective-permute-start | bytes 3145736 | tf_op jit(solution)/shard_map/ppermute | solution.py:604
  197.3 68.0 %collective-permute-start.10 = (bf16[2,1024,384]{2,1,0:T(8,128)(2,1)S(1)}, bf16[2,1024,384]{2,1,0:T(8,128)(2,1)}, u32[]{:S(2)}, u32[]{:S(2)}) collective-permute-start(bf16[2,1024,384]{2,1,0:T(8,128)(2,1)S(1)} %pad_maximum_fusion.rest_4_), channel_id=1, source_target_pairs={{8,16},{12,20},{16,8},{20,12},{9,17},{13,21},{17,9},{21,13},{10,18... | collective-permute-start | bytes 4718600 | tf_op jit(solution)/shard_map/ppermute | solution.py:604
  200.6 17.2 %collective-permute-start.7 = (bf16[2,128,1024]{2,1,0:T(8,128)(2,1)S(1)}, bf16[2,128,1024]{2,1,0:T(8,128)(2,1)S(1)}, u32[]{:S(2)}, u32[]{:S(2)}) collective-permute-start(bf16[2,128,1024]{2,1,0:T(8,128)(2,1)S(1)} %broadcast_select_fusion.1), channel_id=1, source_target_pairs={{8,16},{12,20},{9,17},{13,21},{10,18},{14,22},{11,19},{15,23}} | collective-permute-start | bytes 1572872 | tf_op jit(solution)/shard_map/ppermute | solution.py:604
  217.0 2.4 collective-permute-start.17
  217.8 50.6 %collective-permute-start.2 = (bf16[1040,384]{1,0:T(8,128)(2,1)}, bf16[1040,384]{1,0:T(8,128)(2,1)}, u32[]{:S(2)}, u32[]{:S(2)}) collective-permute-start(bf16[1040,384]{1,0:T(8,128)(2,1)} %collective-permute-done.rest_1_), channel_id=1, source_target_pairs={{8,12},{12,8},{16,20},{20,16},{9,13},{13,9},{17,21},{21,17},{10,14... | collective-permute-start | bytes 2396168 | tf_op jit(solution)/shard_map/ppermute | solution.py:604
  219.4 77.9 %collective-permute-start.9 = (bf16[2,1024,384]{2,1,0:T(8,128)(2,1)S(1)}, bf16[2,1024,384]{2,1,0:T(8,128)(2,1)}, u32[]{:S(2)}, u32[]{:S(2)}) collective-permute-start(bf16[2,1024,384]{2,1,0:T(8,128)(2,1)S(1)} %pad_maximum_fusion.rest_4_), channel_id=1, source_target_pairs={{0,8},{4,12},{24,16},{28,20},{1,9},{5,13},{25,17},{29,21},{2,10},{... | collective-permute-start | bytes 4718600 | tf_op jit(solution)/shard_map/ppermute | solution.py:604
  265.3 64.1 %collective-permute-start.18 = (bf16[2,1024,384]{2,1,0:T(8,128)(2,1)S(1)}, bf16[2,1024,384]{2,1,0:T(8,128)(2,1)}, u32[]{:S(2)}, u32[]{:S(2)}) collective-permute-start(bf16[2,1024,384]{2,1,0:T(8,128)(2,1)S(1)} %pad_maximum_fusion.1.rest_4_), channel_id=1, source_target_pairs={{0,8},{4,12},{24,16},{28,20},{1,9},{5,13},{25,17},{29,21},{2,10},{... | collective-permute-start | bytes 4718600 | tf_op jit(solution)/shard_map/ppermute | solution.py:604
  268.4 6.7 %collective-permute-start.29 = (bf16[2,1024,256]{2,1,0:T(8,128)(2,1)}, bf16[2,1024,256]{2,1,0:T(8,128)(2,1)}, u32[]{:S(2)}, u32[]{:S(2)}) collective-permute-start(bf16[2,1024,256]{2,1,0:T(8,128)(2,1)} %collective-permute-done.27.rest_5_), channel_id=1, source_target_pairs={{8,16},{12,20},{16,8},{20,12},{9,17},{13,21},{17,9},{21,13},{10,18... | collective-permute-start | bytes 3145736 | tf_op jit(solution)/shard_map/ppermute | solution.py:604
  275.2 55.6 %collective-permute-start.8 = (bf16[2,128,1024]{2,1,0:T(8,128)(2,1)}, bf16[2,128,1024]{2,1,0:T(8,128)(2,1)}, u32[]{:S(2)}, u32[]{:S(2)}) collective-permute-start(bf16[2,128,1024]{2,1,0:T(8,128)(2,1)} %broadcast_select_fusion.2), channel_id=1, source_target_pairs={{16,24},{20,28},{17,25},{21,29},{18,26},{22,30},{19,27},{23,31}} | collective-permute-start | bytes 1572872 | tf_op jit(solution)/shard_map/ppermute | solution.py:604
  277.6 82.4 %copy-start.33 = (s32[2]{0:T(128)S(1)}, s32[2]{0:T(128)}, u32[]{:S(2)}) copy-start(s32[2]{0:T(128)} %constant.80.clone) | copy-start | bytes 28
  297.3 34.7 %collective-permute-start.30 = (bf16[1152,256]{1,0:T(8,128)(2,1)}, bf16[1152,256]{1,0:T(8,128)(2,1)S(1)}, u32[]{:S(2)}, u32[]{:S(2)}) collective-permute-start(bf16[1152,256]{1,0:T(8,128)(2,1)} %get-tuple-element.44), channel_id=1, source_target_pairs={{8,12},{12,8},{16,20},{20,16},{9,13},{13,9},{17,21},{21,17},{10,14... | collective-permute-start | bytes 1769480 | tf_op jit(solution)/shard_map/ppermute | solution.py:604
  329.4 18.3 %collective-permute-start.31 = (bf16[1152,256]{1,0:T(8,128)(2,1)}, bf16[1152,256]{1,0:T(8,128)(2,1)S(1)}, u32[]{:S(2)}, u32[]{:S(2)}) collective-permute-start(bf16[1152,256]{1,0:T(8,128)(2,1)} %get-tuple-element.45), channel_id=1, source_target_pairs={{8,0},{12,4},{16,24},{20,28},{9,1},{13,5},{17,25},{21,29},{10,2},{... | collective-permute-start | bytes 1769480 | tf_op jit(solution)/shard_map/ppermute | solution.py:604
  330.7 27.5 %collective-permute-start.32 = (bf16[1152,256]{1,0:T(8,128)(2,1)}, bf16[1152,256]{1,0:T(8,128)(2,1)}, u32[]{:S(2)}, u32[]{:S(2)}) collective-permute-start(bf16[1152,256]{1,0:T(8,128)(2,1)} %get-tuple-element.46), channel_id=1, source_target_pairs={{8,4},{12,0},{16,28},{20,24},{9,5},{13,1},{17,29},{21,25},{10,6},{... | collective-permute-start | bytes 1769480 | tf_op jit(solution)/shard_map/ppermute | solution.py:604
  332.1 49.1 %collective-permute-start.19 = (bf16[2,1024,384]{2,1,0:T(8,128)(2,1)S(1)}, bf16[2,1024,384]{2,1,0:T(8,128)(2,1)S(1)}, u32[]{:S(2)}, u32[]{:S(2)}) collective-permute-start(bf16[2,1024,384]{2,1,0:T(8,128)(2,1)S(1)} %pad_maximum_fusion.1.rest_4_), channel_id=1, source_target_pairs={{8,16},{12,20},{16,8},{20,12},{9,17},{13,21},{17,9},{21,13},{10,18... | collective-permute-start | bytes 4718600 | tf_op jit(solution)/shard_map/ppermute | solution.py:604
  348.6 35.9 %collective-permute-start.20 = (bf16[2,1024,384]{2,1,0:T(8,128)(2,1)}, bf16[2,1024,384]{2,1,0:T(8,128)(2,1)}, u32[]{:S(2)}, u32[]{:S(2)}) collective-permute-start(bf16[2,1024,384]{2,1,0:T(8,128)(2,1)} %collective-permute-done.18.rest_5_), channel_id=1, source_target_pairs={{8,16},{12,20},{16,8},{20,12},{9,17},{13,21},{17,9},{21,13},{10,18... | collective-permute-start | bytes 4718600 | tf_op jit(solution)/shard_map/ppermute | solution.py:604
  358.2 33.8 %collective-permute-start.11 = (bf16[2,1024,384]{2,1,0:T(8,128)(2,1)}, bf16[2,1024,384]{2,1,0:T(8,128)(2,1)}, u32[]{:S(2)}, u32[]{:S(2)}) collective-permute-start(bf16[2,1024,384]{2,1,0:T(8,128)(2,1)} %collective-permute-done.9.rest_5_), channel_id=1, source_target_pairs={{8,16},{12,20},{16,8},{20,12},{9,17},{13,21},{17,9},{21,13},{10,18... | collective-permute-start | bytes 4718600 | tf_op jit(solution)/shard_map/ppermute | solution.py:604
  381.2 1.8 collective-permute-start.35
  383.0 6.6 %collective-permute-start.38 = (bf16[256,256]{1,0:T(8,128)(2,1)}, bf16[256,256]{1,0:T(8,128)(2,1)S(1)}, u32[]{:S(2)}, u32[]{:S(2)}) collective-permute-start(bf16[256,256]{1,0:T(8,128)(2,1)} %get-tuple-element.53), channel_id=1, source_target_pairs={{0,2},{1,3},{2,0},{3,1},{4,6},{5,7},{6,4},{7,5},{8,10},{9,11},{10,... | collective-permute-start | bytes 393224 | tf_op jit(solution)/shard_map/ppermute | solution.py:607
  384.5 6.2 %collective-permute-start.41 = (bf16[256,256]{1,0:T(8,128)(2,1)}, bf16[256,256]{1,0:T(8,128)(2,1)S(1)}, u32[]{:S(2)}, u32[]{:S(2)}) collective-permute-start(bf16[256,256]{1,0:T(8,128)(2,1)} %get-tuple-element.56), channel_id=1, source_target_pairs={{0,3},{1,2},{2,1},{3,0},{4,7},{5,6},{6,5},{7,4},{8,11},{9,10},{10,... | collective-permute-start | bytes 393224 | tf_op jit(solution)/shard_map/ppermute | solution.py:607
  389.6 8.8 %collective-permute-start.21 = (bf16[1120,384]{1,0:T(8,128)(2,1)}, bf16[1120,384]{1,0:T(8,128)(2,1)S(1)}, u32[]{:S(2)}, u32[]{:S(2)}) collective-permute-start(bf16[1120,384]{1,0:T(8,128)(2,1)} %get-tuple-element.39), channel_id=1, source_target_pairs={{8,12},{12,8},{16,20},{20,16},{9,13},{13,9},{17,21},{21,17},{10,14... | collective-permute-start | bytes 2580488 | tf_op jit(solution)/shard_map/ppermute | solution.py:604
  390.7 65.9 %collective-permute-start.22 = (bf16[1120,384]{1,0:T(8,128)(2,1)}, bf16[1120,384]{1,0:T(8,128)(2,1)S(1)}, u32[]{:S(2)}, u32[]{:S(2)}) collective-permute-start(bf16[1120,384]{1,0:T(8,128)(2,1)} %get-tuple-element.40), channel_id=1, source_target_pairs={{8,0},{12,4},{16,24},{20,28},{9,1},{13,5},{17,25},{21,29},{10,2},{... | collective-permute-start | bytes 2580488 | tf_op jit(solution)/shard_map/ppermute | solution.py:604
  392.0 83.1 %collective-permute-start.23 = (bf16[1120,384]{1,0:T(8,128)(2,1)}, bf16[1120,384]{1,0:T(8,128)(2,1)}, u32[]{:S(2)}, u32[]{:S(2)}) collective-permute-start(bf16[1120,384]{1,0:T(8,128)(2,1)} %get-tuple-element.41), channel_id=1, source_target_pairs={{8,4},{12,0},{16,28},{20,24},{9,5},{13,1},{17,29},{21,25},{10,6},{... | collective-permute-start | bytes 2580488 | tf_op jit(solution)/shard_map/ppermute | solution.py:604
  398.3 78.3 %copy-start.13 = (bf16[1120,384]{1,0:T(8,128)(2,1)}, bf16[1120,384]{1,0:T(8,128)(2,1)S(1)}, u32[]{:S(2)}) copy-start(bf16[1120,384]{1,0:T(8,128)(2,1)S(1)} %collective-permute-done.21.rest_1_) | copy-start | bytes 2580484
  398.3 85.1 %collective-permute-start.12 = (bf16[1120,384]{1,0:T(8,128)(2,1)}, bf16[1120,384]{1,0:T(8,128)(2,1)S(1)}, u32[]{:S(2)}, u32[]{:S(2)}) collective-permute-start(bf16[1120,384]{1,0:T(8,128)(2,1)} %get-tuple-element.34), channel_id=1, source_target_pairs={{8,12},{12,8},{16,20},{20,16},{9,13},{13,9},{17,21},{21,17},{10,14... | collective-permute-start | bytes 2580488 | tf_op jit(solution)/shard_map/ppermute | solution.py:604
  456.6 36.9 %collective-permute-start.13 = (bf16[1120,384]{1,0:T(8,128)(2,1)}, bf16[1120,384]{1,0:T(8,128)(2,1)S(1)}, u32[]{:S(2)}, u32[]{:S(2)}) collective-permute-start(bf16[1120,384]{1,0:T(8,128)(2,1)} %get-tuple-element.35), channel_id=1, source_target_pairs={{8,0},{12,4},{16,24},{20,28},{9,1},{13,5},{17,25},{21,29},{10,2},{... | collective-permute-start | bytes 2580488 | tf_op jit(solution)/shard_map/ppermute | solution.py:604
  475.1 36.9 %collective-permute-start.14 = (bf16[1120,384]{1,0:T(8,128)(2,1)}, bf16[1120,384]{1,0:T(8,128)(2,1)}, u32[]{:S(2)}, u32[]{:S(2)}) collective-permute-start(bf16[1120,384]{1,0:T(8,128)(2,1)} %get-tuple-element.36), channel_id=1, source_target_pairs={{8,4},{12,0},{16,28},{20,24},{9,5},{13,1},{17,29},{21,25},{10,6},{... | collective-permute-start | bytes 2580488 | tf_op jit(solution)/shard_map/ppermute | solution.py:604
  483.5 36.5 %collective-permute-start.34 = (bf16[256,384]{1,0:T(8,128)(2,1)}, bf16[256,384]{1,0:T(8,128)(2,1)S(1)}, u32[]{:S(2)}, u32[]{:S(2)}) collective-permute-start(bf16[256,384]{1,0:T(8,128)(2,1)} %get-tuple-element.49), channel_id=1, source_target_pairs={{0,1},{1,0},{2,3},{3,2},{4,5},{5,4},{6,7},{7,6},{8,9},{9,8},{10,11... | collective-permute-start | bytes 589832 | tf_op jit(solution)/shard_map/ppermute | solution.py:607
  493.5 27.4 %collective-permute-start.37 = (bf16[256,384]{1,0:T(8,128)(2,1)}, bf16[256,384]{1,0:T(8,128)(2,1)S(1)}, u32[]{:S(2)}, u32[]{:S(2)}) collective-permute-start(bf16[256,384]{1,0:T(8,128)(2,1)} %get-tuple-element.52), channel_id=1, source_target_pairs={{0,2},{1,3},{2,0},{3,1},{4,6},{5,7},{6,4},{7,5},{8,10},{9,11},{10,... | collective-permute-start | bytes 589832 | tf_op jit(solution)/shard_map/ppermute | solution.py:607
  512.0 9.1 %collective-permute-start.40 = (bf16[256,384]{1,0:T(8,128)(2,1)}, bf16[256,384]{1,0:T(8,128)(2,1)S(1)}, u32[]{:S(2)}, u32[]{:S(2)}) collective-permute-start(bf16[256,384]{1,0:T(8,128)(2,1)} %get-tuple-element.55), channel_id=1, source_target_pairs={{0,3},{1,2},{2,1},{3,0},{4,7},{5,6},{6,5},{7,4},{8,11},{9,10},{10,... | collective-permute-start | bytes 589832 | tf_op jit(solution)/shard_map/ppermute | solution.py:607
  520.0 2.3 collective-permute-start.33
  520.9 8.0 %collective-permute-start.36 = (bf16[256,384]{1,0:T(8,128)(2,1)}, bf16[256,384]{1,0:T(8,128)(2,1)S(1)}, u32[]{:S(2)}, u32[]{:S(2)}) collective-permute-start(bf16[256,384]{1,0:T(8,128)(2,1)} %get-tuple-element.51), channel_id=1, source_target_pairs={{0,2},{1,3},{2,0},{3,1},{4,6},{5,7},{6,4},{7,5},{8,10},{9,11},{10,... | collective-permute-start | bytes 589832 | tf_op jit(solution)/shard_map/ppermute | solution.py:607
  521.1 10.2 %collective-permute-start.39 = (bf16[256,384]{1,0:T(8,128)(2,1)}, bf16[256,384]{1,0:T(8,128)(2,1)S(1)}, u32[]{:S(2)}, u32[]{:S(2)}) collective-permute-start(bf16[256,384]{1,0:T(8,128)(2,1)} %get-tuple-element.54), channel_id=1, source_target_pairs={{0,3},{1,2},{2,1},{3,0},{4,7},{5,6},{6,5},{7,4},{8,11},{9,10},{10,... | collective-permute-start | bytes 589832 | tf_op jit(solution)/shard_map/ppermute | solution.py:607
  (33 other events, 654.7 us)

commit v3 on v2

--- a/solution.py
+++ b/solution.py
@@ -549,37 +549,39 @@
     )(params, near, near_lse, *some)
 
 
-def project(parts, weights, tile=512):
+def project(parts, weights, first_row, so_far=None, tile=512):
     rows = parts[0][0].shape[0]
     width = weights[0].shape[1]
     chunks = len(parts[0])
-    depth = sum(part.shape[1] for part in parts[0])
+    used = sum(part.shape[1] for part in parts[0])
     sides = len(weights)
 
     def body(*refs):
         part_refs = refs[: sides * chunks]
         weight_refs = refs[sides * chunks : sides * chunks + sides]
-        total = jnp.zeros((rows, tile), jnp.float32)
+        total = jnp.zeros((rows, tile), jnp.float32) if so_far is None else refs[-2][...]
         for number, weight in enumerate(weight_refs):
             left = [part_refs[number * chunks + c][...] for c in range(chunks)]
-            left = jnp.concatenate(left, axis=1)
+            left = jnp.concatenate(left, axis=1) if chunks > 1 else left[0]
             total = total + jnp.dot(left, weight[...], preferred_element_type=jnp.float32)
         refs[-1][...] = total.astype(refs[-1].dtype)
 
     flat = [part for group in parts for part in group]
+    extra = [] if so_far is None else [so_far]
+    column = pl.BlockSpec((rows, tile), lambda n: (0, n))
     return pl.pallas_call(
         body,
         grid=(width // tile,),
         in_specs=[pl.BlockSpec(part.shape, lambda n: (0, 0)) for part in flat]
-        + [pl.BlockSpec((depth, tile), lambda n: (0, n))] * sides,
-        out_specs=pl.BlockSpec((rows, tile), lambda n: (0, n)),
-        out_shape=jax.ShapeDtypeStruct((rows, width), jnp.bfloat16),
+        + [pl.BlockSpec((pl.Element(used), pl.Element(tile)), lambda n: (first_row, n * tile))] * sides
+        + [column] * len(extra),
+        out_specs=column,
+        out_shape=jax.ShapeDtypeStruct((rows, width), jnp.float32 if so_far is None else jnp.bfloat16),
         compiler_params=pltpu.CompilerParams(dimension_semantics=("arbitrary",)),
         cost_estimate=pl.CostEstimate(
-            flops=2 * rows * depth * sides * width, bytes_accessed=2 * depth * sides * width, transcendentals=0
+            flops=2 * rows * used * sides * width, bytes_accessed=2 * used * sides * width, transcendentals=0
         ),
-        name="project",
-    )(*flat, *weights)
+    )(*flat, *weights, *extra)
 
 
 def local_columns(queries, key_rows, value_rows, random_owner, random_local, output_weight):
@@ -672,7 +674,8 @@
         for distance, part in enumerate(outs):
             parts[distance].append(swap(part, distance) if distance else part)
     weights = [output_weight, swap(output_weight, 1), far_weight, swap(far_weight, 1)]
-    return project(parts, weights)
+    early = project([part[:1] for part in parts], weights, 0)
+    return project([part[1:] for part in parts], weights, moved[1][0] * HEAD_DIM, early)
 
 
 def local(*arrays):

time: 552 us -> 510 us (0.924)
  starting transfers between devices: 127 us -> 83.3 us
  Pallas kernels: 63.1 us -> 71.6 us
  waiting for transfers between devices: 334 us -> 328 us
    ppermute x33, starting transfers between devices: 115 us -> 74.5 us  [move(): return lax.ppermute(array, 'seq', pairs)]
    ppermute x12, waiting for transfers between devices: 140 us -> 119 us  [swap(): lax.ppermute(array, 'head', [(i, i ^ distance) for i in range(head_count)])]
    ppermute x33, waiting for transfers between devices: 194 us -> 210 us  [move(): return lax.ppermute(array, 'seq', pairs)]
    pallas_call x1 -> x2, Pallas kernels: 17.6 us -> 25.9 us  [project(): pl.pallas_call(body, grid=(width // tile,), in_specs=[pl.BlockSpec(part.s...]
  transfers between devices with their start and end apart: 45 -> 45, of which waited for: 19 -> 13; matrix products, arithmetic and copies ran while one was open for 4% -> 4% of each run, Pallas kernels for 8% -> 11%
where the time goes in v3:
time: 510 us; the launch traced here: 508 us
  waiting for transfers between devices  328 us (64%)
  starting transfers between devices  83.3 us (16%)
  Pallas kernels  71.6 us (14%)
  local copies, waits for them, and re-layouts  13.8 us (3%)
  other arithmetic  9.82 us (2%)
    ppermute x33, waiting for transfers between devices, move(): return lax.ppermute(array, 'seq', pairs)  210 us
    ppermute x12, waiting for transfers between devices, swap(): lax.ppermute(array, 'head', [(i, i ^ distance) for i in range(head_count)])  119 us
    ppermute x33, starting transfers between devices, move(): return lax.ppermute(array, 'seq', pairs)  74.5 us
    pallas_call x2, Pallas kernels, project(): pl.pallas_call(body, grid=(width // tile,), in_specs=[pl.BlockSpec(part.s...  25.9 us
    pallas_call x3, Pallas kernels, merge(): pl.pallas_call(body, grid_spec=pltpu.PrefetchScalarGridSpec(num_scalar_pr...  19.2 us
    pallas_call x3, Pallas kernels, column_attention(): pl.pallas_call(body, grid_spec=pltpu.PrefetchScalarGridSpec(num_scalar_pr...  13.9 us
    pallas_call x1, Pallas kernels, near_attention(): pl.pallas_call(body, grid_spec=pltpu.PrefetchScalarGridSpec(num_scalar_pr...  12.6 us
  transfers between devices with their start and end apart: 45, of which 13 were waited for; matrix products, arithmetic and copies ran while one was open for 4% of the time, Pallas kernels for 11%

profile of v3, /device:TPU:0, one launch (start us, length us, event | category | flops | bytes accessed | tf_op | source)
XLA Modules:
  0.0 507.8 jit_solution(15278171384481798549)
XLA Ops:
  0.0 3.0 collective-permute-start.34
  4.1 4.2 collective-permute-start.5
  9.4 1.3 collective-permute-start.3
  12.9 1.4 collective-permute-start.19
  14.4 1.3 fusion.10
  15.7 14.0 %collective-permute-done.3.before_ref = bf16[2,64,1024]{2,1,0:T(8,128)(2,1)S(1)} collective-permute-done((bf16[2,64,1024]{2,1,0:T(8,128)(2,1)S(1)}, bf16[2,64,1024]{2,1,0:T(8,128)(2,1)S(1)}, u32[]{:S(2)}, u32[]{:S(2)}) %collective-permute-start.3) | collective-permute-done | bytes 262176 | tf_op jit(solution)/shard_map/ppermute | solution.py:606
  29.7 1.6 collective-permute-start.10
  31.2 2.2 collective-permute-start.9
  33.4 2.1 collective-permute-start.18
  37.1 1.6 collective-permute-start.1
  38.7 21.4 %collective-permute-done.18.rest_1_ = bf16[1024,256]{1,0:T(8,128)(2,1)} collective-permute-done((bf16[1024,256]{1,0:T(8,128)(2,1)}, bf16[1024,256]{1,0:T(8,128)(2,1)}, u32[]{:S(2)}, u32[]{:S(2)}) %collective-permute-start.18) | collective-permute-done | bytes 524320 | tf_op jit(solution)/shard_map/ppermute | solution.py:606
  60.0 5.3 %collective-permute-start = (bf16[1040,384]{1,0:T(8,128)(2,1)S(1)}, bf16[1040,384]{1,0:T(8,128)(2,1)}, u32[]{:S(2)}, u32[]{:S(2)}) collective-permute-start(bf16[1040,384]{1,0:T(8,128)(2,1)S(1)} %pad_maximum_fusion.3.rest_0_), channel_id=1, source_target_pairs={{0,8},{4,12},{24,16},{28,20},{1,9},{5,13},{25,17},{29,21},{2,10},{... | collective-permute-start | bytes 2396168 | tf_op jit(solution)/shard_map/ppermute | solution.py:606
  65.5 1.5 collective-permute-start.6
  67.0 116.8 %collective-permute-done.34.refs_6_.refs_10_ = bf16[1024,4096]{1,0:T(8,128)(2,1)} collective-permute-done((bf16[1024,4096]{1,0:T(8,128)(2,1)}, bf16[1024,4096]{1,0:T(8,128)(2,1)}, u32[]{:S(2)}, u32[]{:S(2)}) %collective-permute-start.34) | collective-permute-done | bytes 8388640 | tf_op jit(solution)/shard_map/ppermute | solution.py:609
  186.5 10.1 %collective-permute-start.21 = (bf16[2,1024,256]{2,1,0:T(8,128)(2,1)S(1)}, bf16[2,1024,256]{2,1,0:T(8,128)(2,1)}, u32[]{:S(2)}, u32[]{:S(2)}) collective-permute-start(bf16[2,1024,256]{2,1,0:T(8,128)(2,1)S(1)} %pad_maximum_fusion.2.rest_4_), channel_id=1, source_target_pairs={{0,8},{4,12},{24,16},{28,20},{1,9},{5,13},{25,17},{29,21},{2,10},{... | collective-permute-start | bytes 3145736 | tf_op jit(solution)/shard_map/ppermute | solution.py:606
  197.2 11.3 %collective-permute-start.12 = (bf16[2,1024,384]{2,1,0:T(8,128)(2,1)S(1)}, bf16[2,1024,384]{2,1,0:T(8,128)(2,1)S(1)}, u32[]{:S(2)}, u32[]{:S(2)}) collective-permute-start(bf16[2,1024,384]{2,1,0:T(8,128)(2,1)S(1)} %pad_maximum_fusion.rest_4_), channel_id=1, source_target_pairs={{0,8},{4,12},{24,16},{28,20},{1,9},{5,13},{25,17},{29,21},{2,10},{... | collective-permute-start | bytes 4718600 | tf_op jit(solution)/shard_map/ppermute | solution.py:606
  210.7 8.5 %collective-permute-done.21.rest_5_ = bf16[2,1024,256]{2,1,0:T(8,128)(2,1)} collective-permute-done((bf16[2,1024,256]{2,1,0:T(8,128)(2,1)S(1)}, bf16[2,1024,256]{2,1,0:T(8,128)(2,1)}, u32[]{:S(2)}, u32[]{:S(2)}) %collective-permute-start.21) | collective-permute-done | bytes 1048608 | tf_op jit(solution)/shard_map/ppermute | solution.py:606
  219.9 1.6 collective-permute-start.2
  221.5 1.7 collective-permute-start.23
  223.4 28.5 %collective-permute-done.12.rest_5_ = bf16[2,1024,384]{2,1,0:T(8,128)(2,1)S(1)} collective-permute-done((bf16[2,1024,384]{2,1,0:T(8,128)(2,1)S(1)}, bf16[2,1024,384]{2,1,0:T(8,128)(2,1)S(1)}, u32[]{:S(2)}, u32[]{:S(2)}) %collective-permute-start.12) | collective-permute-done | bytes 1572896 | tf_op jit(solution)/shard_map/ppermute | solution.py:606
  253.0 1.8 collective-permute-start.37
  254.9 6.8 %collective-permute-start.36 = (bf16[2,1024,384]{2,1,0:T(8,128)(2,1)S(1)}, bf16[2,1024,384]{2,1,0:T(8,128)(2,1)}, u32[]{:S(2)}, u32[]{:S(2)}) collective-permute-start(bf16[2,1024,384]{2,1,0:T(8,128)(2,1)S(1)} %pad_maximum_fusion.1.rest_4_), channel_id=1, source_target_pairs={{0,8},{4,12},{24,16},{28,20},{1,9},{5,13},{25,17},{29,21},{2,10},{... | collective-permute-start | bytes 4718600 | tf_op jit(solution)/shard_map/ppermute | solution.py:606
  263.9 2.5 broadcast_select_fusion.2
  267.2 1.5 collective-permute-start.8
  269.9 3.9 shard_map.102
  274.5 18.1 %collective-permute-done.36.rest_5_ = bf16[2,1024,384]{2,1,0:T(8,128)(2,1)} collective-permute-done((bf16[2,1024,384]{2,1,0:T(8,128)(2,1)S(1)}, bf16[2,1024,384]{2,1,0:T(8,128)(2,1)}, u32[]{:S(2)}, u32[]{:S(2)}) %collective-permute-start.36) | collective-permute-done | bytes 1572896 | tf_op jit(solution)/shard_map/ppermute | solution.py:606
  295.2 1.8 collective-permute-start.38
  297.0 19.6 %collective-permute-done.25.rest_2_ = bf16[1152,256]{1,0:T(8,128)(2,1)S(1)} collective-permute-done((bf16[1152,256]{1,0:T(8,128)(2,1)}, bf16[1152,256]{1,0:T(8,128)(2,1)S(1)}, u32[]{:S(2)}, u32[]{:S(2)}) %collective-permute-start.25) | collective-permute-done | bytes 589856 | tf_op jit(solution)/shard_map/ppermute | solution.py:606
  317.4 6.5 %collective-permute-done.26.rest_3_ = bf16[1152,256]{1,0:T(8,128)(2,1)S(1)} collective-permute-done((bf16[1152,256]{1,0:T(8,128)(2,1)}, bf16[1152,256]{1,0:T(8,128)(2,1)S(1)}, u32[]{:S(2)}, u32[]{:S(2)}) %collective-permute-start.26) | collective-permute-done | bytes 589856 | tf_op jit(solution)/shard_map/ppermute | solution.py:606
  324.7 1.8 collective-permute-start.14
  327.2 2.5 broadcast_select_fusion.3.token_ref
  329.6 12.6 %near.1 = (f32[1024,1024]{1,0:T(8,128)}, bf16[1024,128]{1,0:T(8,128)(2,1)}) custom-call(s32[1]{0:T(128)} %bitcast.par, bf16[1024,1024]{1,0:T(8,128)(2,1)} %query_ref.1, bf16[1024,1024]{1,0:T(8,128)(2,1)} %key_ref.1, bf16[1024,1024]{1,0:T(8,128)(2,1)} %value_ref.1, bf16[2,64,1024]{2,1,0:T(8,128)(2,1)} %copy-done.21, bf16[2,64,1024]{2,1,0:T(8,128)(2,1)} %copy-done.22, ...), custom_call_target="tpu_custom_call" | custom-call | flops 1342177280 | bytes 8388608 | tf_op jit(solution)/shard_map/near/pallas_call | solution.py:341
  342.3 5.4 %shard_map.103 = (bf16[256,256]{1,0:T(8,128)(2,1)}, bf16[256,256]{1,0:T(8,128)(2,1)}, bf16[256,256]{1,0:T(8,128)(2,1)}, bf16[256,256]{1,0:T(8,128)(2,1)}) custom-call(s32[267]{0:T(512)} %concatenate.29.par, f32[1024,1024]{1,0:T(8,128)} %get-tuple-element.31.near_ref, bf16[1024,128]{1,0:T(8,128)(2,1)} %get-tuple-element.32.lse_ref, ...), custom_call_target="tpu_custom_call" | custom-call | flops 16777216 | bytes 2097152 | tf_op jit(solution)/shard_map/pallas_call | solution.py:530
  347.8 5.0 shard_map.104
  356.1 5.0 shard_map.100
  362.8 36.7 %collective-permute-done.40.rest_2_ = bf16[1120,384]{1,0:T(8,128)(2,1)} collective-permute-done((bf16[1120,384]{1,0:T(8,128)(2,1)}, bf16[1120,384]{1,0:T(8,128)(2,1)}, u32[]{:S(2)}, u32[]{:S(2)}) %collective-permute-start.40) | collective-permute-done | bytes 860192 | tf_op jit(solution)/shard_map/ppermute | solution.py:606
  400.7 21.5 %collective-permute-done.41.rest_3_ = bf16[1120,384]{1,0:T(8,128)(2,1)} collective-permute-done((bf16[1120,384]{1,0:T(8,128)(2,1)}, bf16[1120,384]{1,0:T(8,128)(2,1)}, u32[]{:S(2)}, u32[]{:S(2)}) %collective-permute-start.41) | collective-permute-done | bytes 860192 | tf_op jit(solution)/shard_map/ppermute | solution.py:606
  422.2 1.5 collective-permute-start.17
  423.7 6.8 %shard_map.105 = (bf16[256,384]{1,0:T(8,128)(2,1)}, bf16[256,384]{1,0:T(8,128)(2,1)}, bf16[256,384]{1,0:T(8,128)(2,1)}, bf16[256,384]{1,0:T(8,128)(2,1)}) custom-call(s32[267]{0:T(512)} %concatenate.29.par, f32[1024,1024]{1,0:T(8,128)} %get-tuple-element.31.near_ref, bf16[1024,128]{1,0:T(8,128)(2,1)} %get-tuple-element.32.lse_ref, ...), custom_call_target="tpu_custom_call" | custom-call | flops 25165824 | bytes 3145728 | tf_op jit(solution)/shard_map/pallas_call | solution.py:530
  430.7 26.4 %collective-permute-done.16.rest_2_ = bf16[1120,384]{1,0:T(8,128)(2,1)S(1)} collective-permute-done((bf16[1120,384]{1,0:T(8,128)(2,1)}, bf16[1120,384]{1,0:T(8,128)(2,1)S(1)}, u32[]{:S(2)}, u32[]{:S(2)}) %collective-permute-start.16) | collective-permute-done | bytes 860192 | tf_op jit(solution)/shard_map/ppermute | solution.py:606
  457.1 1.5 collective-permute-start.43
  458.6 8.6 %collective-permute-done.17.rest_3_ = bf16[1120,384]{1,0:T(8,128)(2,1)S(1)} collective-permute-done((bf16[1120,384]{1,0:T(8,128)(2,1)}, bf16[1120,384]{1,0:T(8,128)(2,1)S(1)}, u32[]{:S(2)}, u32[]{:S(2)}) %collective-permute-start.17) | collective-permute-done | bytes 860192 | tf_op jit(solution)/shard_map/ppermute | solution.py:606
  468.1 7.0 %shard_map.101 = (bf16[256,384]{1,0:T(8,128)(2,1)}, bf16[256,384]{1,0:T(8,128)(2,1)}, bf16[256,384]{1,0:T(8,128)(2,1)}, bf16[256,384]{1,0:T(8,128)(2,1)}) custom-call(s32[267]{0:T(512)} %concatenate.29.par, f32[1024,1024]{1,0:T(8,128)} %get-tuple-element.31.near_ref, bf16[1024,128]{1,0:T(8,128)(2,1)} %get-tuple-element.32.lse_ref, ...), custom_call_target="tpu_custom_call" | custom-call | flops 25165824 | bytes 3145728 | tf_op jit(solution)/shard_map/pallas_call | solution.py:530
  475.2 1.6 collective-permute-start.30
  477.4 1.5 collective-permute-start.29
  479.3 11.2 %shard_map.106.refs_12_ = f32[256,4096]{1,0:T(8,128)} custom-call(bf16[256,384]{1,0:T(8,128)(2,1)} %get-tuple-element.53.refs_0_, bf16[256,384]{1,0:T(8,128)(2,1)} %copy-done.23, bf16[256,384]{1,0:T(8,128)(2,1)} %copy-done.24, bf16[256,384]{1,0:T(8,128)(2,1)} %copy-done.25, bf16[1024,4096]{1,0:T(8,128)(2,1)} %refs_8_.1, ...), custom_call_target="tpu_custom_call" | custom-call | flops 3221225472 | bytes 12582912 | tf_op jit(solution)/shard_map/pallas_call | solution.py:572
  490.5 1.9 collective-permute-done.31.refs_6_
  493.0 14.7 %shard_map.107 = bf16[256,4096]{1,0:T(8,128)(2,1)} custom-call(bf16[256,384]{1,0:T(8,128)(2,1)} %get-tuple-element.37.refs_0_, bf16[256,256]{1,0:T(8,128)(2,1)} %get-tuple-element.42.refs_1_, bf16[256,384]{1,0:T(8,128)(2,1)} %copy-done.26, bf16[256,256]{1,0:T(8,128)(2,1)} %copy-done.29, bf16[256,384]{1,0:T(8,128)(2,1)} %copy-done.27, ...), custom_call_target="tpu_custom_call" | custom-call | flops 5368709120 | bytes 20971520 | tf_op jit(solution)/shard_map/pallas_call | solution.py:572
  (171 shorter events, 32.0 us)
Async XLA Ops:
  0.0 183.8 %collective-permute-start.34 = (bf16[1024,4096]{1,0:T(8,128)(2,1)}, bf16[1024,4096]{1,0:T(8,128)(2,1)}, u32[]{:S(2)}, u32[]{:S(2)}) collective-permute-start(bf16[1024,4096]{1,0:T(8,128)(2,1)} %refs_8_.1), channel_id=1, source_target_pairs={{0,2},{1,3},{2,0},{3,1},{4,6},{5,7},{6,4},{7,5},{8,10},{9,11},{10,... | collective-permute-start | bytes 25165832 | tf_op jit(solution)/shard_map/ppermute | solution.py:609
  4.1 29.3 %collective-permute-start.5 = (bf16[2,128,1024]{2,1,0:T(8,128)(2,1)S(1)}, bf16[2,128,1024]{2,1,0:T(8,128)(2,1)}, u32[]{:S(2)}, u32[]{:S(2)}) collective-permute-start(bf16[2,128,1024]{2,1,0:T(8,128)(2,1)S(1)} %pad_maximum_fusion.4), channel_id=1, source_target_pairs={{0,4},{1,5},{2,6},{3,7}} | collective-permute-start | bytes 1572872 | tf_op jit(solution)/shard_map/ppermute | solution.py:606
  9.4 20.3 %collective-permute-start.3 = (bf16[2,64,1024]{2,1,0:T(8,128)(2,1)S(1)}, bf16[2,64,1024]{2,1,0:T(8,128)(2,1)S(1)}, u32[]{:S(2)}, u32[]{:S(2)}) collective-permute-start(bf16[2,64,1024]{2,1,0:T(8,128)(2,1)S(1)} %pad_maximum_fusion.5), channel_id=1, source_target_pairs={{0,4},{4,8},{8,12},{12,16},{16,20},{20,24},{24,28},{1,5},{5,9},{9,... | collective-permute-start | bytes 786440 | tf_op jit(solution)/shard_map/ppermute | solution.py:606
  10.7 20.5 %collective-permute-start.4 = (bf16[2,64,1024]{2,1,0:T(8,128)(2,1)S(1)}, bf16[2,64,1024]{2,1,0:T(8,128)(2,1)S(1)}, u32[]{:S(2)}, u32[]{:S(2)}) collective-permute-start(bf16[2,64,1024]{2,1,0:T(8,128)(2,1)S(1)} %pad_maximum_fusion.6), channel_id=1, source_target_pairs={{4,0},{8,4},{12,8},{16,12},{20,16},{24,20},{28,24},{5,1},{9,5},{13... | collective-permute-start | bytes 786440 | tf_op jit(solution)/shard_map/ppermute | solution.py:606
  12.9 24.1 %collective-permute-start.19 = (bf16[1024,256]{1,0:T(8,128)(2,1)}, bf16[1024,256]{1,0:T(8,128)(2,1)}, u32[]{:S(2)}, u32[]{:S(2)}) collective-permute-start(bf16[1024,256]{1,0:T(8,128)(2,1)} %slice.76.rest_0_), channel_id=1, source_target_pairs={{8,12},{12,8},{16,20},{20,16},{9,13},{13,9},{17,21},{21,17},{10,14... | collective-permute-start | bytes 1572872 | tf_op jit(solution)/shard_map/ppermute | solution.py:606
  29.7 35.7 %collective-permute-start.10 = (bf16[1024,384]{1,0:T(8,128)(2,1)}, bf16[1024,384]{1,0:T(8,128)(2,1)}, u32[]{:S(2)}, u32[]{:S(2)}) collective-permute-start(bf16[1024,384]{1,0:T(8,128)(2,1)} %get-tuple-element.67.rest_0_), channel_id=1, source_target_pairs={{8,12},{12,8},{16,20},{20,16},{9,13},{13,9},{17,21},{21,17},{10,14... | collective-permute-start | bytes 2359304 | tf_op jit(solution)/shard_map/ppermute | solution.py:606
  31.2 34.3 %collective-permute-start.9 = (bf16[1024,384]{1,0:T(8,128)(2,1)}, bf16[1024,384]{1,0:T(8,128)(2,1)}, u32[]{:S(2)}, u32[]{:S(2)}) collective-permute-start(bf16[1024,384]{1,0:T(8,128)(2,1)} %get-tuple-element.67.rest_0_), channel_id=1, source_target_pairs={{0,8},{4,12},{24,16},{28,20},{1,9},{5,13},{25,17},{29,21},{2,10},{... | collective-permute-start | bytes 2359304 | tf_op jit(solution)/shard_map/ppermute | solution.py:606
  33.4 26.6 %collective-permute-start.18 = (bf16[1024,256]{1,0:T(8,128)(2,1)}, bf16[1024,256]{1,0:T(8,128)(2,1)}, u32[]{:S(2)}, u32[]{:S(2)}) collective-permute-start(bf16[1024,256]{1,0:T(8,128)(2,1)} %slice.76.rest_0_), channel_id=1, source_target_pairs={{0,8},{4,12},{24,16},{28,20},{1,9},{5,13},{25,17},{29,21},{2,10},{... | collective-permute-start | bytes 1572872 | tf_op jit(solution)/shard_map/ppermute | solution.py:606
  37.1 148.0 %copy-start.6 = (bf16[1040,384]{1,0:T(8,128)(2,1)}, bf16[1040,384]{1,0:T(8,128)(2,1)S(1)}, u32[]{:S(2)}) copy-start(bf16[1040,384]{1,0:T(8,128)(2,1)S(1)} %pad_maximum_fusion.3.rest_0_) | copy-start | bytes 2396164
  37.1 148.0 %collective-permute-start.1 = (bf16[1040,384]{1,0:T(8,128)(2,1)S(1)}, bf16[1040,384]{1,0:T(8,128)(2,1)}, u32[]{:S(2)}, u32[]{:S(2)}) collective-permute-start(bf16[1040,384]{1,0:T(8,128)(2,1)S(1)} %pad_maximum_fusion.3.rest_0_), channel_id=1, source_target_pairs={{8,12},{12,8},{16,20},{20,16},{9,13},{13,9},{17,21},{21,17},{10,14... | collective-permute-start | bytes 2396168 | tf_op jit(solution)/shard_map/ppermute | solution.py:606
  60.0 125.7 %collective-permute-start = (bf16[1040,384]{1,0:T(8,128)(2,1)S(1)}, bf16[1040,384]{1,0:T(8,128)(2,1)}, u32[]{:S(2)}, u32[]{:S(2)}) collective-permute-start(bf16[1040,384]{1,0:T(8,128)(2,1)S(1)} %pad_maximum_fusion.3.rest_0_), channel_id=1, source_target_pairs={{0,8},{4,12},{24,16},{28,20},{1,9},{5,13},{25,17},{29,21},{2,10},{... | collective-permute-start | bytes 2396168 | tf_op jit(solution)/shard_map/ppermute | solution.py:606
  65.4 131.2 %copy-start.1 = (bf16[1024,1024]{1,0:T(8,128)(2,1)S(1)}, bf16[1024,1024]{1,0:T(8,128)(2,1)}, u32[]{:S(2)}) copy-start(bf16[1024,1024]{1,0:T(8,128)(2,1)} %value_ref.1) | copy-start | bytes 6291460
  65.4 412.0 %collective-permute-start.33 = (bf16[1024,4096]{1,0:T(8,128)(2,1)}, bf16[1024,4096]{1,0:T(8,128)(2,1)}, u32[]{:S(2)}, u32[]{:S(2)}) collective-permute-start(bf16[1024,4096]{1,0:T(8,128)(2,1)} %refs_8_.1), channel_id=1, source_target_pairs={{0,1},{1,0},{2,3},{3,2},{4,5},{5,4},{6,7},{7,6},{8,9},{9,8},{10,11... | collective-permute-start | bytes 25165832 | tf_op jit(solution)/shard_map/ppermute | solution.py:609
  65.5 121.0 %collective-permute-start.6 = (bf16[2,128,1024]{2,1,0:T(8,128)(2,1)S(1)}, bf16[2,128,1024]{2,1,0:T(8,128)(2,1)S(1)}, u32[]{:S(2)}, u32[]{:S(2)}) collective-permute-start(bf16[2,128,1024]{2,1,0:T(8,128)(2,1)S(1)} %broadcast_select_fusion), channel_id=1, source_target_pairs={{0,8},{4,12},{1,9},{5,13},{2,10},{6,14},{3,11},{7,15}} | collective-permute-start | bytes 1572872 | tf_op jit(solution)/shard_map/ppermute | solution.py:606
  183.8 295.2 %collective-permute-start.35 = (bf16[1024,4096]{1,0:T(8,128)(2,1)}, bf16[1024,4096]{1,0:T(8,128)(2,1)}, u32[]{:S(2)}, u32[]{:S(2)}) collective-permute-start(bf16[1024,4096]{1,0:T(8,128)(2,1)} %collective-permute-done.34.refs_6_.refs_10_), channel_id=1, source_target_pairs={{0,1},{1,0},{2,3},{3,2},{4,5},{5,4},{6,7},{7,6},{8,9},{9,8},{10,11... | collective-permute-start | bytes 25165832 | tf_op jit(solution)/shard_map/ppermute | solution.py:609
  185.0 24.9 %collective-permute-start.22 = (bf16[2,1024,256]{2,1,0:T(8,128)(2,1)S(1)}, bf16[2,1024,256]{2,1,0:T(8,128)(2,1)S(1)}, u32[]{:S(2)}, u32[]{:S(2)}) collective-permute-start(bf16[2,1024,256]{2,1,0:T(8,128)(2,1)S(1)} %pad_maximum_fusion.2.rest_4_), channel_id=1, source_target_pairs={{8,16},{12,20},{16,8},{20,12},{9,17},{13,21},{17,9},{21,13},{10,18... | collective-permute-start | bytes 3145736 | tf_op jit(solution)/shard_map/ppermute | solution.py:606
  185.8 11.4 %collective-permute-start.20 = (bf16[1024,256]{1,0:T(8,128)(2,1)}, bf16[1024,256]{1,0:T(8,128)(2,1)S(1)}, u32[]{:S(2)}, u32[]{:S(2)}) collective-permute-start(bf16[1024,256]{1,0:T(8,128)(2,1)} %collective-permute-done.18.rest_1_), channel_id=1, source_target_pairs={{8,12},{12,8},{16,20},{20,16},{9,13},{13,9},{17,21},{21,17},{10,14... | collective-permute-start | bytes 1572872 | tf_op jit(solution)/shard_map/ppermute | solution.py:606
  186.5 32.7 %collective-permute-start.21 = (bf16[2,1024,256]{2,1,0:T(8,128)(2,1)S(1)}, bf16[2,1024,256]{2,1,0:T(8,128)(2,1)}, u32[]{:S(2)}, u32[]{:S(2)}) collective-permute-start(bf16[2,1024,256]{2,1,0:T(8,128)(2,1)S(1)} %pad_maximum_fusion.2.rest_4_), channel_id=1, source_target_pairs={{0,8},{4,12},{24,16},{28,20},{1,9},{5,13},{25,17},{29,21},{2,10},{... | collective-permute-start | bytes 3145736 | tf_op jit(solution)/shard_map/ppermute | solution.py:606
  197.2 119.4 %copy-start.3 = (bf16[2,1024,384]{2,1,0:T(8,128)(2,1)}, bf16[2,1024,384]{2,1,0:T(8,128)(2,1)S(1)}, u32[]{:S(2)}) copy-start(bf16[2,1024,384]{2,1,0:T(8,128)(2,1)S(1)} %pad_maximum_fusion.rest_4_) | copy-start | bytes 4718596
  197.2 54.7 %collective-permute-start.12 = (bf16[2,1024,384]{2,1,0:T(8,128)(2,1)S(1)}, bf16[2,1024,384]{2,1,0:T(8,128)(2,1)S(1)}, u32[]{:S(2)}, u32[]{:S(2)}) collective-permute-start(bf16[2,1024,384]{2,1,0:T(8,128)(2,1)S(1)} %pad_maximum_fusion.rest_4_), channel_id=1, source_target_pairs={{0,8},{4,12},{24,16},{28,20},{1,9},{5,13},{25,17},{29,21},{2,10},{... | collective-permute-start | bytes 4718600 | tf_op jit(solution)/shard_map/ppermute | solution.py:606
  210.0 9.9 %collective-permute-start.7 = (bf16[2,128,1024]{2,1,0:T(8,128)(2,1)S(1)}, bf16[2,128,1024]{2,1,0:T(8,128)(2,1)S(1)}, u32[]{:S(2)}, u32[]{:S(2)}) collective-permute-start(bf16[2,128,1024]{2,1,0:T(8,128)(2,1)S(1)} %broadcast_select_fusion.1), channel_id=1, source_target_pairs={{8,16},{12,20},{9,17},{13,21},{10,18},{14,22},{11,19},{15,23}} | collective-permute-start | bytes 1572872 | tf_op jit(solution)/shard_map/ppermute | solution.py:606
  219.2 2.3 collective-permute-start.11
  219.9 34.9 %collective-permute-start.2 = (bf16[1040,384]{1,0:T(8,128)(2,1)}, bf16[1040,384]{1,0:T(8,128)(2,1)}, u32[]{:S(2)}, u32[]{:S(2)}) collective-permute-start(bf16[1040,384]{1,0:T(8,128)(2,1)} %collective-permute-done.rest_1_), channel_id=1, source_target_pairs={{8,12},{12,8},{16,20},{20,16},{9,13},{13,9},{17,21},{21,17},{10,14... | collective-permute-start | bytes 2396168 | tf_op jit(solution)/shard_map/ppermute | solution.py:606
  221.5 45.7 %collective-permute-start.23 = (bf16[2,1024,256]{2,1,0:T(8,128)(2,1)}, bf16[2,1024,256]{2,1,0:T(8,128)(2,1)}, u32[]{:S(2)}, u32[]{:S(2)}) collective-permute-start(bf16[2,1024,256]{2,1,0:T(8,128)(2,1)} %collective-permute-done.21.rest_5_), channel_id=1, source_target_pairs={{8,16},{12,20},{16,8},{20,12},{9,17},{13,21},{17,9},{21,13},{10,18... | collective-permute-start | bytes 3145736 | tf_op jit(solution)/shard_map/ppermute | solution.py:606
  253.0 20.7 %collective-permute-start.37 = (bf16[2,1024,384]{2,1,0:T(8,128)(2,1)S(1)}, bf16[2,1024,384]{2,1,0:T(8,128)(2,1)}, u32[]{:S(2)}, u32[]{:S(2)}) collective-permute-start(bf16[2,1024,384]{2,1,0:T(8,128)(2,1)S(1)} %pad_maximum_fusion.1.rest_4_), channel_id=1, source_target_pairs={{8,16},{12,20},{16,8},{20,12},{9,17},{13,21},{17,9},{21,13},{10,18... | collective-permute-start | bytes 4718600 | tf_op jit(solution)/shard_map/ppermute | solution.py:606
  254.9 37.7 %collective-permute-start.36 = (bf16[2,1024,384]{2,1,0:T(8,128)(2,1)S(1)}, bf16[2,1024,384]{2,1,0:T(8,128)(2,1)}, u32[]{:S(2)}, u32[]{:S(2)}) collective-permute-start(bf16[2,1024,384]{2,1,0:T(8,128)(2,1)S(1)} %pad_maximum_fusion.1.rest_4_), channel_id=1, source_target_pairs={{0,8},{4,12},{24,16},{28,20},{1,9},{5,13},{25,17},{29,21},{2,10},{... | collective-permute-start | bytes 4718600 | tf_op jit(solution)/shard_map/ppermute | solution.py:606
  267.2 26.6 %collective-permute-start.8 = (bf16[2,128,1024]{2,1,0:T(8,128)(2,1)}, bf16[2,128,1024]{2,1,0:T(8,128)(2,1)}, u32[]{:S(2)}, u32[]{:S(2)}) collective-permute-start(bf16[2,128,1024]{2,1,0:T(8,128)(2,1)} %broadcast_select_fusion.2), channel_id=1, source_target_pairs={{16,24},{20,28},{17,25},{21,29},{18,26},{22,30},{19,27},{23,31}} | collective-permute-start | bytes 1572872 | tf_op jit(solution)/shard_map/ppermute | solution.py:606
  273.8 21.4 %collective-permute-start.24 = (bf16[1152,256]{1,0:T(8,128)(2,1)}, bf16[1152,256]{1,0:T(8,128)(2,1)S(1)}, u32[]{:S(2)}, u32[]{:S(2)}) collective-permute-start(bf16[1152,256]{1,0:T(8,128)(2,1)} %get-tuple-element.39), channel_id=1, source_target_pairs={{8,12},{12,8},{16,20},{20,16},{9,13},{13,9},{17,21},{21,17},{10,14... | collective-permute-start | bytes 1769480 | tf_op jit(solution)/shard_map/ppermute | solution.py:606
  292.6 24.0 %collective-permute-start.25 = (bf16[1152,256]{1,0:T(8,128)(2,1)}, bf16[1152,256]{1,0:T(8,128)(2,1)S(1)}, u32[]{:S(2)}, u32[]{:S(2)}) collective-permute-start(bf16[1152,256]{1,0:T(8,128)(2,1)} %get-tuple-element.40), channel_id=1, source_target_pairs={{8,0},{12,4},{16,24},{20,28},{9,1},{13,5},{17,25},{21,29},{10,2},{... | collective-permute-start | bytes 1769480 | tf_op jit(solution)/shard_map/ppermute | solution.py:606
  293.9 30.0 %collective-permute-start.26 = (bf16[1152,256]{1,0:T(8,128)(2,1)}, bf16[1152,256]{1,0:T(8,128)(2,1)S(1)}, u32[]{:S(2)}, u32[]{:S(2)}) collective-permute-start(bf16[1152,256]{1,0:T(8,128)(2,1)} %get-tuple-element.41), channel_id=1, source_target_pairs={{8,4},{12,0},{16,28},{20,24},{9,5},{13,1},{17,29},{21,25},{10,6},{... | collective-permute-start | bytes 1769480 | tf_op jit(solution)/shard_map/ppermute | solution.py:606
  295.2 52.5 %collective-permute-start.38 = (bf16[2,1024,384]{2,1,0:T(8,128)(2,1)}, bf16[2,1024,384]{2,1,0:T(8,128)(2,1)}, u32[]{:S(2)}, u32[]{:S(2)}) collective-permute-start(bf16[2,1024,384]{2,1,0:T(8,128)(2,1)} %collective-permute-done.36.rest_5_), channel_id=1, source_target_pairs={{8,16},{12,20},{16,8},{20,12},{9,17},{13,21},{17,9},{21,13},{10,18... | collective-permute-start | bytes 4718600 | tf_op jit(solution)/shard_map/ppermute | solution.py:606
  316.6 36.1 %collective-permute-start.13 = (bf16[2,1024,384]{2,1,0:T(8,128)(2,1)S(1)}, bf16[2,1024,384]{2,1,0:T(8,128)(2,1)S(1)}, u32[]{:S(2)}, u32[]{:S(2)}) collective-permute-start(bf16[2,1024,384]{2,1,0:T(8,128)(2,1)S(1)} %pad_maximum_fusion.rest_4_), channel_id=1, source_target_pairs={{8,16},{12,20},{16,8},{20,12},{9,17},{13,21},{17,9},{21,13},{10,18... | collective-permute-start | bytes 4718600 | tf_op jit(solution)/shard_map/ppermute | solution.py:606
  324.7 30.1 %collective-permute-start.14 = (bf16[2,1024,384]{2,1,0:T(8,128)(2,1)}, bf16[2,1024,384]{2,1,0:T(8,128)(2,1)}, u32[]{:S(2)}, u32[]{:S(2)}) collective-permute-start(bf16[2,1024,384]{2,1,0:T(8,128)(2,1)} %copy-done.8), channel_id=1, source_target_pairs={{8,16},{12,20},{16,8},{20,12},{9,17},{13,21},{17,9},{21,13},{10,18... | collective-permute-start | bytes 4718600 | tf_op jit(solution)/shard_map/ppermute | solution.py:606
  347.7 5.8 %collective-permute-start.28 = (bf16[256,256]{1,0:T(8,128)(2,1)}, bf16[256,256]{1,0:T(8,128)(2,1)S(1)}, u32[]{:S(2)}, u32[]{:S(2)}) collective-permute-start(bf16[256,256]{1,0:T(8,128)(2,1)} %get-tuple-element.44), channel_id=1, source_target_pairs={{0,1},{1,0},{2,3},{3,2},{4,5},{5,4},{6,7},{7,6},{8,9},{9,8},{10,11... | collective-permute-start | bytes 393224 | tf_op jit(solution)/shard_map/ppermute | solution.py:609
  352.8 8.4 %collective-permute-start.39 = (bf16[1120,384]{1,0:T(8,128)(2,1)}, bf16[1120,384]{1,0:T(8,128)(2,1)S(1)}, u32[]{:S(2)}, u32[]{:S(2)}) collective-permute-start(bf16[1120,384]{1,0:T(8,128)(2,1)} %get-tuple-element.50), channel_id=1, source_target_pairs={{8,12},{12,8},{16,20},{20,16},{9,13},{13,9},{17,21},{21,17},{10,14... | collective-permute-start | bytes 2580488 | tf_op jit(solution)/shard_map/ppermute | solution.py:606
  353.5 45.9 %collective-permute-start.40 = (bf16[1120,384]{1,0:T(8,128)(2,1)}, bf16[1120,384]{1,0:T(8,128)(2,1)}, u32[]{:S(2)}, u32[]{:S(2)}) collective-permute-start(bf16[1120,384]{1,0:T(8,128)(2,1)} %get-tuple-element.51), channel_id=1, source_target_pairs={{8,0},{12,4},{16,24},{20,28},{9,1},{13,5},{17,25},{21,29},{10,2},{... | collective-permute-start | bytes 2580488 | tf_op jit(solution)/shard_map/ppermute | solution.py:606
  354.8 67.4 %collective-permute-start.41 = (bf16[1120,384]{1,0:T(8,128)(2,1)}, bf16[1120,384]{1,0:T(8,128)(2,1)}, u32[]{:S(2)}, u32[]{:S(2)}) collective-permute-start(bf16[1120,384]{1,0:T(8,128)(2,1)} %get-tuple-element.52), channel_id=1, source_target_pairs={{8,4},{12,0},{16,28},{20,24},{9,5},{13,1},{17,29},{21,25},{10,6},{... | collective-permute-start | bytes 2580488 | tf_op jit(solution)/shard_map/ppermute | solution.py:606
  362.1 68.5 %collective-permute-start.15 = (bf16[1120,384]{1,0:T(8,128)(2,1)}, bf16[1120,384]{1,0:T(8,128)(2,1)S(1)}, u32[]{:S(2)}, u32[]{:S(2)}) collective-permute-start(bf16[1120,384]{1,0:T(8,128)(2,1)} %get-tuple-element.34), channel_id=1, source_target_pairs={{8,12},{12,8},{16,20},{20,16},{9,13},{13,9},{17,21},{21,17},{10,14... | collective-permute-start | bytes 2580488 | tf_op jit(solution)/shard_map/ppermute | solution.py:606
  399.4 57.6 %collective-permute-start.16 = (bf16[1120,384]{1,0:T(8,128)(2,1)}, bf16[1120,384]{1,0:T(8,128)(2,1)S(1)}, u32[]{:S(2)}, u32[]{:S(2)}) collective-permute-start(bf16[1120,384]{1,0:T(8,128)(2,1)} %get-tuple-element.35), channel_id=1, source_target_pairs={{8,0},{12,4},{16,24},{20,28},{9,1},{13,5},{17,25},{21,29},{10,2},{... | collective-permute-start | bytes 2580488 | tf_op jit(solution)/shard_map/ppermute | solution.py:606
  422.2 45.0 %collective-permute-start.17 = (bf16[1120,384]{1,0:T(8,128)(2,1)}, bf16[1120,384]{1,0:T(8,128)(2,1)S(1)}, u32[]{:S(2)}, u32[]{:S(2)}) collective-permute-start(bf16[1120,384]{1,0:T(8,128)(2,1)} %get-tuple-element.36), channel_id=1, source_target_pairs={{8,4},{12,0},{16,28},{20,24},{9,5},{13,1},{17,29},{21,25},{10,6},{... | collective-permute-start | bytes 2580488 | tf_op jit(solution)/shard_map/ppermute | solution.py:606
  430.6 44.5 %collective-permute-start.42 = (bf16[256,384]{1,0:T(8,128)(2,1)}, bf16[256,384]{1,0:T(8,128)(2,1)S(1)}, u32[]{:S(2)}, u32[]{:S(2)}) collective-permute-start(bf16[256,384]{1,0:T(8,128)(2,1)} %get-tuple-element.54), channel_id=1, source_target_pairs={{0,1},{1,0},{2,3},{3,2},{4,5},{5,4},{6,7},{7,6},{8,9},{9,8},{10,11... | collective-permute-start | bytes 589832 | tf_op jit(solution)/shard_map/ppermute | solution.py:609
  457.1 19.7 %collective-permute-start.43 = (bf16[256,384]{1,0:T(8,128)(2,1)}, bf16[256,384]{1,0:T(8,128)(2,1)S(1)}, u32[]{:S(2)}, u32[]{:S(2)}) collective-permute-start(bf16[256,384]{1,0:T(8,128)(2,1)} %get-tuple-element.55), channel_id=1, source_target_pairs={{0,2},{1,3},{2,0},{3,1},{4,6},{5,7},{6,4},{7,5},{8,10},{9,11},{10,... | collective-permute-start | bytes 589832 | tf_op jit(solution)/shard_map/ppermute | solution.py:609
  467.2 10.2 %collective-permute-start.44 = (bf16[256,384]{1,0:T(8,128)(2,1)}, bf16[256,384]{1,0:T(8,128)(2,1)S(1)}, u32[]{:S(2)}, u32[]{:S(2)}) collective-permute-start(bf16[256,384]{1,0:T(8,128)(2,1)} %get-tuple-element.56), channel_id=1, source_target_pairs={{0,3},{1,2},{2,1},{3,0},{4,7},{5,6},{6,5},{7,4},{8,11},{9,10},{10,... | collective-permute-start | bytes 589832 | tf_op jit(solution)/shard_map/ppermute | solution.py:609
  475.2 15.3 %collective-permute-start.30 = (bf16[256,256]{1,0:T(8,128)(2,1)S(1)}, bf16[256,256]{1,0:T(8,128)(2,1)S(1)}, u32[]{:S(2)}, u32[]{:S(2)}) collective-permute-start(bf16[256,256]{1,0:T(8,128)(2,1)S(1)} %copy-done.35), channel_id=1, source_target_pairs={{0,2},{1,3},{2,0},{3,1},{4,6},{5,7},{6,4},{7,5},{8,10},{9,11},{10,... | collective-permute-start | bytes 393224 | tf_op jit(solution)/shard_map/ppermute | solution.py:609
  476.7 13.7 %collective-permute-start.32 = (bf16[256,256]{1,0:T(8,128)(2,1)S(1)}, bf16[256,256]{1,0:T(8,128)(2,1)S(1)}, u32[]{:S(2)}, u32[]{:S(2)}) collective-permute-start(bf16[256,256]{1,0:T(8,128)(2,1)S(1)} %copy-done.34), channel_id=1, source_target_pairs={{0,3},{1,2},{2,1},{3,0},{4,7},{5,6},{6,5},{7,4},{8,11},{9,10},{10,... | collective-permute-start | bytes 393224 | tf_op jit(solution)/shard_map/ppermute | solution.py:609
  477.4 13.1 %collective-permute-start.27 = (bf16[256,384]{1,0:T(8,128)(2,1)}, bf16[256,384]{1,0:T(8,128)(2,1)S(1)}, u32[]{:S(2)}, u32[]{:S(2)}) collective-permute-start(bf16[256,384]{1,0:T(8,128)(2,1)} %get-tuple-element.43), channel_id=1, source_target_pairs={{0,1},{1,0},{2,3},{3,2},{4,5},{5,4},{6,7},{7,6},{8,9},{9,8},{10,11... | collective-permute-start | bytes 589832 | tf_op jit(solution)/shard_map/ppermute | solution.py:609
  477.4 13.1 %collective-permute-start.29 = (bf16[256,384]{1,0:T(8,128)(2,1)}, bf16[256,384]{1,0:T(8,128)(2,1)S(1)}, u32[]{:S(2)}, u32[]{:S(2)}) collective-permute-start(bf16[256,384]{1,0:T(8,128)(2,1)} %get-tuple-element.45), channel_id=1, source_target_pairs={{0,2},{1,3},{2,0},{3,1},{4,6},{5,7},{6,4},{7,5},{8,10},{9,11},{10,... | collective-permute-start | bytes 589832 | tf_op jit(solution)/shard_map/ppermute | solution.py:609
  479.0 13.4 %collective-permute-start.31 = (bf16[256,384]{1,0:T(8,128)(2,1)}, bf16[256,384]{1,0:T(8,128)(2,1)S(1)}, u32[]{:S(2)}, u32[]{:S(2)}) collective-permute-start(bf16[256,384]{1,0:T(8,128)(2,1)} %get-tuple-element.47), channel_id=1, source_target_pairs={{0,3},{1,2},{2,1},{3,0},{4,7},{5,6},{6,5},{7,4},{8,11},{9,10},{10,... | collective-permute-start | bytes 589832 | tf_op jit(solution)/shard_map/ppermute | solution.py:609
  (36 other events, 527.6 us)
